TPU v7x, 32 devices: a whole 2x2x4 slice. The times are simulated.
32 devices in a mesh: row: 8 (over z, core), col: 2 (over x), gz: 2 (over y).
Axes of the slice: x: 2, y: 2, z: 4, core: 2. Of those that a mesh axis runs over, the one named last changes fastest.
Arguments:
- initial_field: float32 [8, 32, 32, 256], P(None, 'row', 'col', 'gz'), may hold values from -6 to 6
- source_term: float32 [8, 32, 32, 256], P(None, 'row', 'col', 'gz'), may hold values from -6 to 6
- cell_class: int32 [32, 32, 256], P('row', 'col', 'gz'), may hold values from 0 to 15
- class_shift: float32 [16], replicated, may hold values from 0.05 to 4
- surface_cell: int32 [4096], P(('row', 'col', 'gz')), may hold values from 0 to 8191
- live_count: int32 [32], P(('row', 'col', 'gz')), may hold values from 1 to 128, 2560 in all
- panel_geometry: float32 [4, 4096], P(None, ('row', 'col', 'gz')), may hold values from 0.5 to 2
Outputs:
- final_field: float32 [8, 32, 32, 256], P(None, 'row', 'col', 'gz')
- boundary_potential: float32 [8, 4096], P(None, ('row', 'col', 'gz'))
Inputs may be any that keep to these rules, and one draw needn't show every extreme that they name: Slots 0 to live_count[b] - 1 of brick b are in use; the counts sum to 2560. `surface_cell`: A cell index inside the panel's own brick, x * 16 * 128 + y * 128 + z.
All inputs are finite; a program needn't handle non-finite values. No bound on the sum of `live_count` on one device may be relied on, other than what follows from the above.
Results may differ from a plain program's by a relative error of at most 0.004.
Values may be sent and summed in bfloat16 or wider, within the bound.
A program may use at most 128 MiB of HBM per device.

v0:
```python
import functools
import math

import jax
import jax.numpy as jnp
import numpy as np
from jax import lax
from jax.experimental import pallas as pl
from jax.experimental.pallas import tpu as pltpu
from jax.sharding import PartitionSpec as P

SWEEPS = 3
ROUNDS = 2
STEPS = SWEEPS * ROUNDS

relax_weight = 0.8
wave_number = 25.0
soften = 0.05
coupling = 0.5

MESH = pl.DeviceIdType.MESH
AXES = ("row", "col", "gz")


def cosine_terms(degree=8):
    nodes = 0.125 * (1.0 + np.cos(np.pi * (np.arange(64) + 0.5) / 64))
    fitted = np.polynomial.Polynomial.fit(
        nodes, np.cos(2 * np.pi * np.sqrt(nodes)), degree, domain=[0.0, 0.25]
    )
    return [float(c) for c in fitted.convert().coef]


COSINE = cosine_terms()


def cosine_of_turns(turns):
    fraction = turns - jnp.floor(turns + 0.5)
    square = fraction * fraction
    value = jnp.full_like(square, COSINE[-1])
    for term in reversed(COSINE[:-1]):
        value = value * square + term
    return value


def kernel(
    sizes,
    init_hbm, source_hbm, class_hbm, shift_hbm, cell_hbm, geo_hbm, live_ref,
    field_ref, potential_ref,
    init_v, source_v, class_v, weight_v, state_v, forcing_v,
    x_out, x_in, y_out, y_in, z_out, z_in,
    geo_all, column_v, tile_v, density_out, density_all,
    shift_ref, cell_ref, geo_ref,
    local_sem, face_send, face_recv, geo_sem, density_sem,
):
    rows, cols, depths = sizes
    devices = rows * cols * depths
    channels, size_x, size_y, size_z = init_hbm.shape
    slots = cell_hbm.shape[1]
    classes = shift_ref.shape[0]
    factor = 1.0 / math.sqrt(slots * devices)
    here = tuple(lax.axis_index(axis) for axis in AXES)
    me = (here[0] * cols + here[1]) * depths + here[2]

    copies = [
        pltpu.make_async_copy(init_hbm, init_v, local_sem.at[0]),
        pltpu.make_async_copy(class_hbm, class_v, local_sem.at[1]),
        pltpu.make_async_copy(source_hbm, source_v, local_sem.at[2]),
        pltpu.make_async_copy(geo_hbm, geo_ref, local_sem.at[3]),
        pltpu.make_async_copy(shift_hbm, shift_ref, local_sem.at[4]),
        pltpu.make_async_copy(cell_hbm, cell_ref, local_sem.at[5]),
    ]
    for copy in copies:
        copy.start()

    def each_other(action):
        def at(a, first):
            row = lax.rem(here[0] + a, rows)
            for b in range(cols):
                for c in range(depths):
                    if first and b == 0 and c == 0:
                        continue
                    action((row, lax.rem(here[1] + b, cols), lax.rem(here[2] + c, depths)))

        def others(i, carry):
            at(i, False)
            return carry

        lax.fori_loop(1, rows, others, 0)
        at(0, True)

    barrier = pltpu.get_barrier_semaphore()
    each_other(
        lambda device: pl.semaphore_signal(barrier, inc=1, device_id=device, device_id_type=MESH)
    )

    lane = lax.broadcasted_iota(jnp.int32, (size_y, size_z), 1)
    line = lax.broadcasted_iota(jnp.int32, (size_y, size_z), 0)
    pair = lane >> 1
    edge = (lane == 0) | (lane == size_z - 1)

    def pack(k, e, x, value, packed):
        if x == 0:
            x_out[k, 0, e] = value.astype(x_out.dtype)
        if x == size_x - 1:
            x_out[k, 1, e] = value.astype(x_out.dtype)
        y_out[k, 0, e, x : x + 1, :] = value[0:1, :]
        y_out[k, 1, e, x : x + 1, :] = value[size_y - 1 : size_y, :]
        at = e * size_x + x
        return jnp.where(pair == at, pltpu.roll(value, lax.rem(2 * at + 1, size_z), 1), packed)

    def face_copies(k):
        made = []
        for axis, (send, receive) in enumerate(((x_out, x_in), (y_out, y_in), (z_out, z_in))):
            count = sizes[axis]
            if count == 1:
                continue
            for up in (0, 1):
                target = {AXES[axis]: here[axis] + (1 if up else -1)}
                source = send.at[k] if axis == 2 else send.at[k, up]
                copy = pltpu.make_async_remote_copy(
                    src_ref=source,
                    dst_ref=receive.at[k, 1 - up],
                    send_sem=face_send.at[k, 2 * axis + up],
                    recv_sem=face_recv.at[k, 2 * axis + 1 - up],
                    device_id=target,
                    device_id_type=MESH,
                )
                sends = here[axis] < count - 1 if up else here[axis] > 0
                gets = here[axis] > 0 if up else here[axis] < count - 1
                made.append((copy, sends, gets))
        return made

    def start_faces(k):
        for copy, sends, _ in face_copies(k):
            pl.when(sends)(copy.start)

    def await_faces(k):
        for copy, _, gets in face_copies(k):
            pl.when(gets)(copy.wait_recv)

    def finish_faces(k):
        for copy, sends, _ in face_copies(k):
            pl.when(sends)(copy.wait_send)

    x_in[STEPS] = jnp.zeros(x_in.shape[1:], x_in.dtype)
    y_in[STEPS] = jnp.zeros(y_in.shape[1:], y_in.dtype)
    z_in[STEPS] = jnp.zeros(z_in.shape[1:], z_in.dtype)

    copies[0].wait()

    def pack_first(e, packed):
        for x in range(size_x):
            packed = pack(0, e, x, init_v[e, x], packed)
        return packed

    z_out[0] = lax.fori_loop(
        0, channels, pack_first, jnp.zeros((size_y, size_z), jnp.float32), unroll=True
    )

    copies[3].wait()
    eye = lax.broadcasted_iota(jnp.int32, (slots, slots), 0) == lax.broadcasted_iota(
        jnp.int32, (slots, slots), 1
    )
    for i in range(3):
        column = jnp.sum(jnp.where(eye, geo_ref[i : i + 1, :], 0.0), axis=1, keepdims=True)
        column_v[i] = jnp.broadcast_to(column, (slots, slots))
    geo_all[me] = geo_ref[...]

    pl.semaphore_wait(barrier, devices - 1)
    start_faces(0)

    def gather_copy(source, gathered, sems, device):
        return pltpu.make_async_remote_copy(
            src_ref=source,
            dst_ref=gathered.at[me],
            send_sem=sems.at[0],
            recv_sem=sems.at[1],
            device_id=device,
            device_id_type=MESH,
        )

    def start_gather(source, gathered, sems):
        each_other(lambda device: gather_copy(source, gathered, sems, device).start())

    def await_gather(gathered, sems, which):
        whole = gathered.at[pl.ds(0, devices - 1)]
        pltpu.make_async_copy(whole, whole, sems.at[which]).wait()

    start_gather(geo_ref, geo_all, geo_sem)

    copies[1].wait()
    copies[4].wait()
    for x in range(size_x):
        kind = class_v[x]
        shift = jnp.zeros(kind.shape, jnp.float32)
        for level in range(classes):
            shift = jnp.where(kind == level, shift_ref[level], shift)
        weight_v[x] = relax_weight / (6.0 + shift)

    copies[5].wait()
    cell = cell_ref[...]
    bits = size_z.bit_length() - 1
    cell_z = cell & (size_z - 1)
    cell_xy = cell >> bits
    pick_z = lax.broadcasted_iota(jnp.int32, (size_z, slots), 0) == cell_z
    pick_z = jnp.where(pick_z, 1.0, 0.0).astype(jnp.bfloat16)
    pick_xy = lax.broadcasted_iota(jnp.int32, (size_x * size_y, slots), 0) == cell_xy
    live = lax.broadcasted_iota(jnp.int32, (channels, slots), 1) < live_ref[0]
    which = lax.broadcasted_iota(jnp.int32, (channels, slots), 0)
    copies[2].wait()

    def now(k, e, x):
        return init_v[e, x] if k == 0 else state_v[k - 1, e, x]

    def inner(k):
        force = source_v if k <= SWEEPS else forcing_v

        def body(e, carry):
            tiles = [now(k, e, x) for x in range(size_x)]
            for x in range(size_x):
                value = tiles[x]
                around = force[e, x]
                if x + 1 < size_x:
                    around = around + tiles[x + 1]
                if x > 0:
                    around = around + tiles[x - 1]
                around = around + jnp.where(
                    line == size_y - 1, 0.0, pltpu.roll(value, size_y - 1, 0)
                )
                around = around + jnp.where(line == 0, 0.0, pltpu.roll(value, 1, 0))
                around = around + jnp.where(
                    lane == size_z - 1, 0.0, pltpu.roll(value, size_z - 1, 1)
                )
                around = around + jnp.where(lane == 0, 0.0, pltpu.roll(value, 1, 1))
                state_v[k, e, x] = (1.0 - relax_weight) * value + weight_v[x] * around
            return carry

        lax.fori_loop(0, channels, body, 0, unroll=8)

    def outer(k):
        last = k == STEPS - 1
        slot = []
        for axis in range(3):
            below = jnp.where(here[axis] > 0, k, STEPS)
            above = jnp.where(here[axis] < sizes[axis] - 1, k, STEPS)
            slot.append((below, above))
        beyond = jnp.where(
            (lane & 1) == 0, z_in[slot[2][0], 0], pltpu.roll(z_in[slot[2][1], 1], size_z - 2, 1)
        )

        def body(e, packed):
            for x in range(size_x):
                low = y_in[slot[1][0], 0, e, x : x + 1, :]
                high = y_in[slot[1][1], 1, e, x : x + 1, :]
                at = e * size_x + x
                around = jnp.where(
                    edge, pltpu.roll(beyond, lax.rem(2 * size_z - 2 * at, size_z), 1), 0.0
                )
                around = around + jnp.where(
                    line == 0, low, jnp.where(line == size_y - 1, high, 0.0)
                )
                if x == 0:
                    around = around + x_in[slot[0][0], 0, e].astype(jnp.float32)
                if x == size_x - 1:
                    around = around + x_in[slot[0][1], 1, e].astype(jnp.float32)
                result = state_v[k, e, x] + weight_v[x] * around
                if last:
                    field_ref[e, x] = result
                else:
                    state_v[k, e, x] = result
                    packed = pack(k + 1, e, x, result, packed)
            return packed

        packed = lax.fori_loop(
            0, channels, body, jnp.zeros((size_y, size_z), jnp.float32), unroll=8
        )
        if not last:
            z_out[k + 1] = packed

    pieces = 4
    chunk = slots // pieces

    def make_tiles(first, stop):
        def body(s, carry):
            source = geo_all[s]
            values = []
            for piece in range(pieces):
                span = slice(piece * chunk, (piece + 1) * chunk)
                delta_x = column_v[0, span, :] - source[0:1, :]
                delta_y = column_v[1, span, :] - source[1:2, :]
                delta_z = column_v[2, span, :] - source[2:3, :]
                distance = jnp.sqrt(delta_x * delta_x + delta_y * delta_y + delta_z * delta_z)
                wave = cosine_of_turns(distance * (wave_number / (2.0 * math.pi)))
                value = (source[3:4, :] * factor) * wave / (distance + soften)
                values.append(value)
            turned = jnp.concatenate(values, axis=0).T
            tile_v[pl.ds(pl.multiple_of(s * slots, slots), slots), :] = turned.astype(tile_v.dtype)
            return carry

        lax.fori_loop(first, stop, body, 0)

    group = math.gcd(devices, 8)

    def apply_tiles(gathered):
        def body(i, total):
            values = jnp.concatenate([gathered[i * group + j] for j in range(group)], axis=1)
            span = pl.ds(pl.multiple_of(i * group * slots, group * slots), group * slots)
            return total + jnp.dot(values, tile_v[span, :], preferred_element_type=jnp.float32)

        return lax.fori_loop(
            0, devices // group, body, jnp.zeros((channels, slots), jnp.float32)
        )

    cut = [0, devices // 4, devices // 2, devices]
    for k in range(STEPS):
        if k != SWEEPS:
            inner(k)
        if k == 1:
            await_gather(geo_all, geo_sem, 1)
        if k in (1, 2):
            make_tiles(cut[k - 1], cut[k])
        await_faces(k)
        outer(k)
        end = k % SWEEPS == SWEEPS - 1
        if k + 1 < STEPS:
            start_faces(k + 1)
        if not end:
            continue
        r = k // SWEEPS
        ending = field_ref if k == STEPS - 1 else state_v.at[k]
        flat = ending[...].reshape(channels * size_x * size_y, size_z).astype(jnp.bfloat16)
        picked = jnp.dot(flat, pick_z, preferred_element_type=jnp.float32)
        density = jnp.zeros((channels, slots), jnp.float32)
        for e in range(channels):
            block = picked[e * size_x * size_y : (e + 1) * size_x * size_y]
            found = jnp.sum(jnp.where(pick_xy, block, 0.0), axis=0, keepdims=True)
            density = jnp.where(which == e, found, density)
        density = jnp.where(live, density, 0.0).astype(jnp.bfloat16)
        density_out[r] = density
        density_all[r, me] = density
        start_gather(density_out.at[r], density_all.at[r], density_sem.at[r])
        if r < ROUNDS - 1:
            inner(k + 1)
        if r == 0:
            make_tiles(cut[2], cut[3])
        await_gather(density_all.at[r], density_sem.at[r], 1)
        potential = jnp.where(live, apply_tiles(density_all.at[r]), 0.0)
        if r == ROUNDS - 1:
            potential_ref[...] = potential
        else:
            half_of = coupling * potential
            big = half_of.astype(jnp.bfloat16).astype(jnp.float32)
            small = half_of - big
            for e in range(channels):
                load = jnp.zeros((size_x * size_y, size_z), jnp.float32)
                for part in (big, small):
                    placed = jnp.where(pick_xy, part[e : e + 1, :], 0.0).astype(jnp.bfloat16)
                    load = load + lax.dot_general(
                        placed, pick_z, (((1,), (1,)), ((), ())),
                        preferred_element_type=jnp.float32,
                    )
                load = load.reshape(size_x, size_y, size_z)
                forcing_v[e] = source_v[e] + load
                state_v[k + 1, e] = state_v[k + 1, e] + weight_v[...] * load

    for k in range(STEPS):
        finish_faces(k)
    await_gather(geo_all, geo_sem, 0)
    for r in range(ROUNDS):
        await_gather(density_all.at[r], density_sem.at[r], 0)


def local(sizes, initial_field, source_term, cell_class, class_shift, surface_cell, live_count,
          panel_geometry):
    channels, size_x, size_y, size_z = initial_field.shape
    slots = surface_cell.shape[0]
    devices = sizes[0] * sizes[1] * sizes[2]
    brick = (channels, size_x, size_y, size_z)
    vmem = pl.BlockSpec(memory_space=pltpu.VMEM)
    hbm = pl.BlockSpec(memory_space=pltpu.HBM)
    per_device = slots * (2 * slots + 4 * 8 + ROUNDS * 2 * channels)
    grant = devices * per_device + 24 * 4 * math.prod(brick)
    operands = [
        pltpu.with_memory_space_constraint(array, pltpu.HBM)
        for array in (
            initial_field, source_term, cell_class, class_shift,
            surface_cell.reshape(1, slots), panel_geometry,
        )
    ]
    operands.append(live_count)
    return pl.pallas_call(
        functools.partial(kernel, sizes),
        out_shape=(
            jax.ShapeDtypeStruct(brick, jnp.float32),
            jax.ShapeDtypeStruct((channels, slots), jnp.float32),
        ),
        in_specs=[hbm] * 6 + [pl.BlockSpec(memory_space=pltpu.SMEM)],
        out_specs=(vmem, vmem),
        scratch_shapes=[
            pltpu.VMEM(brick, jnp.float32),
            pltpu.VMEM(brick, jnp.float32),
            pltpu.VMEM(brick[1:], jnp.int32),
            pltpu.VMEM(brick[1:], jnp.float32),
            pltpu.VMEM((STEPS,) + brick, jnp.float32),
            pltpu.VMEM(brick, jnp.float32),
            pltpu.VMEM((STEPS, 2, channels, size_y, size_z), jnp.bfloat16),
            pltpu.VMEM((STEPS + 1, 2, channels, size_y, size_z), jnp.bfloat16),
            pltpu.VMEM((STEPS, 2, channels, size_x, size_z), jnp.float32),
            pltpu.VMEM((STEPS + 1, 2, channels, size_x, size_z), jnp.float32),
            pltpu.VMEM((STEPS, size_y, size_z), jnp.float32),
            pltpu.VMEM((STEPS + 1, 2, size_y, size_z), jnp.float32),
            pltpu.VMEM((devices, 4, slots), jnp.float32),
            pltpu.VMEM((3, slots, slots), jnp.float32),
            pltpu.VMEM((devices * slots, slots), jnp.bfloat16),
            pltpu.VMEM((ROUNDS, channels, slots), jnp.bfloat16),
            pltpu.VMEM((ROUNDS, devices, channels, slots), jnp.bfloat16),
            pltpu.SMEM(class_shift.shape, jnp.float32),
            pltpu.VMEM((1, slots), jnp.int32),
            pltpu.VMEM(panel_geometry.shape, jnp.float32),
            pltpu.SemaphoreType.DMA((6,)),
            pltpu.SemaphoreType.DMA((STEPS, 6)),
            pltpu.SemaphoreType.DMA((STEPS, 6)),
            pltpu.SemaphoreType.DMA((2,)),
            pltpu.SemaphoreType.DMA((ROUNDS, 2)),
        ],
        compiler_params=pltpu.CompilerParams(
            collective_id=0, has_side_effects=True, vmem_limit_bytes=grant
        ),
    )(*operands)


def solution(mesh):
    placed = (
        P(None, "row", "col", "gz"),
        P(None, "row", "col", "gz"),
        P("row", "col", "gz"),
        P(),
        P(("row", "col", "gz")),
        P(("row", "col", "gz")),
        P(None, ("row", "col", "gz")),
    )
    return jax.shard_map(
        functools.partial(local, tuple(mesh.shape[axis] for axis in AXES)),
        mesh=mesh,
        in_specs=placed,
        out_specs=(P(None, "row", "col", "gz"), P(None, ("row", "col", "gz"))),
        check_vma=False,
    )
```

profile of v0, /device:TPU:0, one launch (start us, length us, event | category | flops | bytes accessed | tf_op | source)
XLA Modules:
  0.0 37.0 jit_solution(1488213874003501266)
XLA Ops:
  1.3 34.5 %shard_map.86 = (f32[8,4,16,128]{3,2,1,0:T(8,128)S(1)}, f32[8,128]{1,0:T(8,128)S(1)}) custom-call(f32[8,4,16,128]{3,2,1,0:T(8,128)} %init_hbm.1, f32[8,4,16,128]{3,2,1,0:T(8,128)} %source_hbm.1, s32[4,16,128]{2,1,0:T(8,128)} %class_hbm.1, f32[16]{0:T(128)} %shift_hbm.1, s32[1,128]{1,0:T(1,128)} %bitcast.1, f32[4,128]{1,0:T(4,128)} %geo_hbm.1, ...), custom_call_target="tpu_custom_call" | custom-call | tf_op jit(solution)/shard_map/pallas_call | solution.py:391
  35.7 0.7 %copy.12 = f32[8,4,16,128]{3,2,1,0:T(8,128)} copy(f32[8,4,16,128]{3,2,1,0:T(8,128)S(1)} %get-tuple-element.4) | data formatting | bytes 524288
  36.4 0.6 %copy.13 = f32[8,128]{1,0:T(8,128)} copy(f32[8,128]{1,0:T(8,128)S(1)} %get-tuple-element.5) | data formatting | bytes 8192
where the time goes:
time: 37.2 us; the launch traced here: 37 us
  Pallas kernels  34.5 us (93%)
  local copies, waits for them, and re-layouts  1.3 us (3%)
  between operations  1.29 us (3%)
    pallas_call x1, Pallas kernels, local(): pl.pallas_call(functools.partial(kernel, sizes), out_shape=(jax.ShapeDtyp...  34.5 us
    unnamed x2, local copies, waits for them, and re-layouts  1.3 us

commit v1 on v0

v1 whole, which is shorter than its diff:
```python
import functools
import math

import jax
import jax.numpy as jnp
import numpy as np
from jax import lax
from jax.experimental import pallas as pl
from jax.experimental.pallas import tpu as pltpu
from jax.sharding import PartitionSpec as P

SWEEPS = 3
ROUNDS = 2
STEPS = SWEEPS * ROUNDS

relax_weight = 0.8
wave_number = 25.0
soften = 0.05
coupling = 0.5

MESH = pl.DeviceIdType.MESH
AXES = ("row", "col", "gz")


def cosine_terms(degree=6):
    nodes = 0.125 * (1.0 + np.cos(np.pi * (np.arange(64) + 0.5) / 64))
    fitted = np.polynomial.Polynomial.fit(
        nodes, np.cos(2 * np.pi * np.sqrt(nodes)), degree, domain=[0.0, 0.25]
    )
    return [float(c) for c in fitted.convert().coef]


COSINE = cosine_terms()


def cosine_of_turns(turns):
    fraction = turns - jnp.floor(turns + 0.5)
    square = fraction * fraction
    value = jnp.full_like(square, COSINE[-1])
    for term in reversed(COSINE[:-1]):
        value = value * square + term
    return value


def kernel(
    sizes,
    init_hbm, source_hbm, class_hbm, shift_hbm, cell_hbm, live_hbm, geo_hbm,
    field_ref, potential_ref,
    init_v, source_v, forcing_v, class_v, weight_v, state_v,
    x_out, x_in, y_out, y_in, z_out, z_in,
    geo_all, column_v, tile_v, density_out, density_all, at_cell,
    shift_ref, live_ref, cell_ref, geo_ref,
    local_sem, face_send, face_recv, gather_send, geo_recv, density_recv,
):
    rows, cols, depths = sizes
    devices = rows * cols * depths
    group = cols * depths
    channels, size_x, size_y, size_z = init_hbm.shape
    slots = cell_hbm.shape[1]
    classes = shift_ref.shape[0]
    factor = 1.0 / math.sqrt(slots * devices)
    here = tuple(lax.axis_index(axis) for axis in AXES)
    me = (here[0] * cols + here[1]) * depths + here[2]

    def brick_copies(hbm, vmem, sem):
        return [
            pltpu.make_async_copy(hbm.at[e], vmem.at[:, :, e, :], sem) for e in range(channels)
        ]

    def brick_wait(vmem, sem):
        pltpu.make_async_copy(vmem, vmem, sem).wait()

    copies = [
        pltpu.make_async_copy(class_hbm, class_v, local_sem.at[1]),
        pltpu.make_async_copy(geo_hbm, geo_ref, local_sem.at[3]),
        pltpu.make_async_copy(shift_hbm, shift_ref, local_sem.at[4]),
        pltpu.make_async_copy(cell_hbm, cell_ref, local_sem.at[5]),
        pltpu.make_async_copy(live_hbm, live_ref, local_sem.at[6]),
    ]
    for copy in brick_copies(init_hbm, init_v, local_sem.at[0]):
        copy.start()
    for copy in copies:
        copy.start()

    def nth(k):
        below, above = here[0], rows - 1 - here[0]
        near = here[0] + jnp.where(lax.rem(k, 2) == 1, (k + 1) // 2, -(k // 2))
        far = jnp.where(below < above, k, rows - 1 - k)
        return jnp.where((k <= 2 * below) & (k <= 2 * above), near, far)

    def each_other(action):
        def at(row, first):
            for b in reversed(range(cols)):
                for c in reversed(range(depths)):
                    if first and b == 0 and c == 0:
                        continue
                    action((row, lax.rem(here[1] + b, cols), lax.rem(here[2] + c, depths)))

        def others(i, carry):
            at(nth(rows - 1 - i), False)
            return carry

        lax.fori_loop(0, rows - 1, others, 0)
        at(here[0], True)

    barrier = pltpu.get_barrier_semaphore()
    each_other(
        lambda device: pl.semaphore_signal(barrier, inc=1, device_id=device, device_id_type=MESH)
    )
    for copy in brick_copies(source_hbm, source_v, local_sem.at[2]):
        copy.start()

    cell_shape = (channels, size_z)
    lane = lax.broadcasted_iota(jnp.int32, cell_shape, 1)
    pair = lane >> 1
    edge = (lane == 0) | (lane == size_z - 1)
    slab = (size_y * channels, size_z)
    slab_lane = lax.broadcasted_iota(jnp.int32, slab, 1)

    def pack(k, x, values, packed):
        if x == 0 or x == size_x - 1:
            for y in range(0, size_y, 2):
                both = jnp.concatenate([values[y], values[y + 1]], axis=0).astype(x_out.dtype)
                if x == 0:
                    x_out[k, 0, y // 2] = both
                if x == size_x - 1:
                    x_out[k, 1, y // 2] = both
        half = pl.ds(channels * (x % 2), channels)
        y_out[k, 0, x // 2, half, :] = values[0].astype(y_out.dtype)
        y_out[k, 1, x // 2, half, :] = values[size_y - 1].astype(y_out.dtype)
        for y in range(size_y):
            at = x * size_y + y
            turned = pltpu.roll(values[y], (2 * at + 1) % size_z, 1)
            packed = jnp.where(pair == at, turned, packed)
        return packed

    def face_copies(k):
        made = []
        for axis, (send, receive) in enumerate(((x_out, x_in), (y_out, y_in), (z_out, z_in))):
            count = sizes[axis]
            if count == 1:
                continue
            for up in (0, 1):
                target = {AXES[axis]: here[axis] + (1 if up else -1)}
                source = send.at[k] if axis == 2 else send.at[k, up]
                side = 0 if count == 2 else 1 - up
                copy = functools.partial(
                    pltpu.make_async_remote_copy,
                    src_ref=source,
                    dst_ref=receive.at[k, 1 - up],
                    send_sem=face_send.at[0],
                    recv_sem=face_recv.at[k % 2, 2 * axis + side],
                    device_id=target,
                    device_id_type=MESH,
                )
                landed = receive.at[k, up]
                got = functools.partial(
                    pltpu.make_async_copy,
                    landed,
                    landed,
                    face_recv.at[k % 2, 2 * axis + (0 if count == 2 else up)],
                )
                exists = here[axis] < count - 1 if up else here[axis] > 0
                made.append((copy, got, exists))
        return made

    def start_faces(k):
        for copy, _, exists in face_copies(k):
            pl.when(exists)(lambda copy=copy: copy().start())

    def await_faces(k):
        for _, got, exists in face_copies(k):
            pl.when(exists)(lambda got=got: got().wait())

    def finish_faces(k):
        for copy, _, exists in face_copies(k):
            pl.when(exists)(lambda copy=copy: copy().wait_send())

    x_in[STEPS] = jnp.zeros(x_in.shape[1:], x_in.dtype)
    y_in[STEPS] = jnp.zeros(y_in.shape[1:], y_in.dtype)
    z_in[STEPS] = jnp.zeros(z_in.shape[1:], z_in.dtype)

    with jax.named_scope("w_init"):
        brick_wait(init_v, local_sem.at[0])

    packed = jnp.zeros(cell_shape, jnp.float32)
    for x in range(size_x):
        packed = pack(0, x, [init_v[x, y] for y in range(size_y)], packed)
    z_out[0] = packed

    copies[1].wait()
    eye = lax.broadcasted_iota(jnp.int32, (slots, slots), 0) == lax.broadcasted_iota(
        jnp.int32, (slots, slots), 1
    )
    for i in range(3):
        column = jnp.sum(jnp.where(eye, geo_ref[i : i + 1, :], 0.0), axis=1, keepdims=True)
        column_v[i] = jnp.broadcast_to(column, (slots, slots))
    geo_all[me] = geo_ref[...]

    with jax.named_scope("w_barrier"):
        pl.semaphore_wait(barrier, devices - 1)
    start_faces(0)

    def start_gather(source, gathered, sem):
        def send(device):
            pltpu.make_async_remote_copy(
                src_ref=source,
                dst_ref=gathered.at[me],
                send_sem=gather_send.at[0],
                recv_sem=sem,
                device_id=device,
                device_id_type=MESH,
            ).start()

        each_other(send)

    def await_gather(gathered, count, sem):
        whole = gathered.at[pl.ds(0, count)]
        pltpu.make_async_copy(whole, whole, sem).wait()

    with jax.named_scope("st_geo"):
        start_gather(geo_ref, geo_all, geo_recv.at[0])

    copies[0].wait()
    copies[2].wait()
    for x in range(size_x):
        kind = class_v[x]
        shift = jnp.zeros(kind.shape, jnp.float32)
        for level in range(classes):
            shift = jnp.where(kind == level, shift_ref[level], shift)
        weight = relax_weight / (6.0 + shift)
        weight_v[x] = jnp.broadcast_to(weight[:, None, :], (size_y, channels, size_z))

    copies[3].wait()
    copies[4].wait()
    cell = cell_ref[...]
    bits = size_z.bit_length() - 1
    cell_z = cell & (size_z - 1)
    cell_xy = cell >> bits
    pick_z = lax.broadcasted_iota(jnp.int32, (size_z, slots), 0) == cell_z
    pick_z = jnp.where(pick_z, 1.0, 0.0).astype(jnp.bfloat16)
    for at in range(size_x * size_y):
        at_cell[at] = jnp.broadcast_to(
            jnp.where(cell_xy == at, 1.0, 0.0), (channels, slots)
        )
    live = lax.broadcasted_iota(jnp.int32, (channels, slots), 1) < live_ref[...]
    brick_wait(source_v, local_sem.at[2])

    def now(k, x):
        return init_v[x] if k == 0 else state_v[k - 1, x]

    def inner(k):
        force = source_v if k <= SWEEPS else forcing_v
        blank = jnp.zeros((1,) + cell_shape, jnp.float32)
        for x in range(size_x):
            value = now(k, x)
            around = force[x]
            if x + 1 < size_x:
                around = around + now(k, x + 1)
            if x > 0:
                around = around + now(k, x - 1)
            around = around + jnp.concatenate([value[1:], blank], axis=0)
            around = around + jnp.concatenate([blank, value[:-1]], axis=0)
            flat = value.reshape(slab)
            beside = jnp.where(slab_lane == size_z - 1, 0.0, pltpu.roll(flat, size_z - 1, 1))
            beside = beside + jnp.where(slab_lane == 0, 0.0, pltpu.roll(flat, 1, 1))
            around = around + beside.reshape(value.shape)
            state_v[k, x] = (1.0 - relax_weight) * value + weight_v[x] * around

    def outer(k):
        last = k == STEPS - 1
        slot = []
        for axis in range(3):
            below = jnp.where(here[axis] > 0, k, STEPS)
            above = jnp.where(here[axis] < sizes[axis] - 1, k, STEPS)
            slot.append((below, above))
        beyond = jnp.where(
            (lane & 1) == 0, z_in[slot[2][0], 0], pltpu.roll(z_in[slot[2][1], 1], size_z - 2, 1)
        )
        packed = jnp.zeros(cell_shape, jnp.float32)
        for x in range(size_x):
            results = []
            for y in range(size_y):
                at = x * size_y + y
                around = jnp.where(
                    edge, pltpu.roll(beyond, (2 * size_z - 2 * at) % size_z, 1), 0.0
                )
                half = slice(channels * (y % 2), channels * (y % 2 + 1))
                if x == 0:
                    around = around + x_in[slot[0][0], 0, y // 2].astype(jnp.float32)[half]
                if x == size_x - 1:
                    around = around + x_in[slot[0][1], 1, y // 2].astype(jnp.float32)[half]
                half = slice(channels * (x % 2), channels * (x % 2 + 1))
                if y == 0:
                    around = around + y_in[slot[1][0], 0, x // 2].astype(jnp.float32)[half]
                if y == size_y - 1:
                    around = around + y_in[slot[1][1], 1, x // 2].astype(jnp.float32)[half]
                result = state_v[k, x, y] + weight_v[x, y] * around
                if last:
                    field_ref[x, y] = result
                else:
                    state_v[k, x, y] = result
                results.append(result)
            if not last:
                packed = pack(k + 1, x, results, packed)
        if not last:
            z_out[k + 1] = packed

    pieces = 4
    chunk = slots // pieces

    def make_tiles(first, stop):
        def body(q, carry):
            for j in range(group):
                source = geo_all[q * group + j]
                for piece in range(pieces):
                    span = slice(piece * chunk, (piece + 1) * chunk)
                    delta_x = column_v[0, span, :] - source[0:1, :]
                    delta_y = column_v[1, span, :] - source[1:2, :]
                    delta_z = column_v[2, span, :] - source[2:3, :]
                    square = delta_x * delta_x + delta_y * delta_y + delta_z * delta_z + 1e-30
                    distance = square * lax.rsqrt(square)
                    wave = cosine_of_turns(distance * (wave_number / (2.0 * math.pi)))
                    value = (source[3:4, :] * factor) * wave / (distance + soften)
                    tile_v[q, span, j * slots : (j + 1) * slots] = value.astype(tile_v.dtype)
            return carry

        lax.fori_loop(first, stop, body, 0)

    def apply_tiles(r):
        total = jnp.zeros((channels, slots), jnp.float32)
        for k in range(rows):
            q = nth(k)
            with jax.named_scope(f"w_dens{r}_{k}"):
                await_gather(density_all.at[r], group - (k == 0), density_recv.at[r, q])
            values = jnp.concatenate(
                [density_all[r, q * group + j] for j in range(group)], axis=1
            )
            total = total + lax.dot_general(
                values, tile_v[q], (((1,), (1,)), ((), ())), preferred_element_type=jnp.float32
            )
        return total

    for k in range(STEPS):
        if k != SWEEPS:
            with jax.named_scope(f"inner{k}"):
                inner(k)
        if k == 2:
            with jax.named_scope("w_geogather"):
                await_gather(geo_all, devices - 1, geo_recv.at[0])
            with jax.named_scope("tilesA"):
                make_tiles(0, rows // 4)
        with jax.named_scope(f"w_faces{k}"):
            await_faces(k)
        with jax.named_scope(f"outer{k}"):
            outer(k)
        end = k % SWEEPS == SWEEPS - 1
        if k + 1 < STEPS:
            start_faces(k + 1)
        if not end:
            continue
        r = k // SWEEPS
        with jax.named_scope(f"density{r}"):
            ending = field_ref if k == STEPS - 1 else state_v.at[k]
            flat = ending[...].reshape(size_x * size_y * channels, size_z).astype(jnp.bfloat16)
            picked = jnp.dot(flat, pick_z, preferred_element_type=jnp.float32)
            picked = picked.reshape(size_x * size_y, channels, slots)
            density = jnp.sum(picked * at_cell[...], axis=0)
            density = jnp.where(live, density, 0.0).astype(jnp.bfloat16)
            density_out[r] = density
            density_all[r, me] = density
        with jax.named_scope(f"st_dens{r}"):
            start_gather(density_out.at[r], density_all.at[r], density_recv.at[r, here[0]])
        if r < ROUNDS - 1:
            with jax.named_scope(f"inner{k+1}"):
                inner(k + 1)
        if r == 0:
            with jax.named_scope("tilesB"):
                make_tiles(rows // 4, rows)
        with jax.named_scope(f"apply{r}"):
            potential = jnp.where(live, apply_tiles(r), 0.0)
        if r == ROUNDS - 1:
            potential_ref[...] = potential
        else:
            with jax.named_scope(f"load{r}"):
                half_of = coupling * potential
                big = half_of.astype(jnp.bfloat16).astype(jnp.float32)
                small = half_of - big
                load = jnp.zeros((size_x * size_y * channels, size_z), jnp.float32)
                for part in (big, small):
                    placed = (at_cell[...] * part[None]).astype(jnp.bfloat16)
                    load = load + lax.dot_general(
                        placed.reshape(size_x * size_y * channels, slots), pick_z,
                        (((1,), (1,)), ((), ())), preferred_element_type=jnp.float32,
                    )
                load = load.reshape(size_x, size_y, channels, size_z)
                forcing_v[...] = source_v[...] + load
                state_v[k + 1] = state_v[k + 1] + weight_v[...] * load

    with jax.named_scope("finish"):
        for k in range(STEPS):
            finish_faces(k)
        await_gather(geo_all, devices - 1, gather_send.at[0])
        for r in range(ROUNDS):
            await_gather(density_all.at[r], devices - 1, gather_send.at[0])


def place(field_v, potential_v, field_hbm, potential_hbm, sem):
    channels = field_hbm.shape[0]
    copies = [
        pltpu.make_async_copy(field_v.at[:, :, e, :], field_hbm.at[e], sem.at[0])
        for e in range(channels)
    ]
    copies.append(pltpu.make_async_copy(potential_v, potential_hbm, sem.at[1]))
    for copy in copies:
        copy.start()
    pltpu.make_async_copy(field_v, field_v, sem.at[0]).wait()
    copies[-1].wait()


def local(sizes, initial_field, source_term, cell_class, class_shift, surface_cell, live_count,
          panel_geometry):
    channels, size_x, size_y, size_z = initial_field.shape
    slots = surface_cell.shape[0]
    rows, cols, depths = sizes
    devices, group = rows * cols * depths, cols * depths
    brick = (size_x, size_y, channels, size_z)
    vmem = pl.BlockSpec(memory_space=pltpu.VMEM)
    hbm = pl.BlockSpec(memory_space=pltpu.HBM)
    per_device = slots * (2 * slots + 4 * 8 + ROUNDS * 2 * 2 * channels)
    grant = devices * per_device + 24 * 4 * math.prod(brick)
    operands = [
        pltpu.with_memory_space_constraint(array, pltpu.HBM)
        for array in (
            initial_field, source_term, cell_class, class_shift,
            surface_cell.reshape(1, slots), panel_geometry,
        )
    ]
    operands.insert(5, live_count.reshape(1, 1))
    two = 2 * channels
    field, potential = pl.pallas_call(
        functools.partial(kernel, sizes),
        out_shape=(
            jax.ShapeDtypeStruct(brick, jnp.float32),
            jax.ShapeDtypeStruct((channels, slots), jnp.float32),
        ),
        in_specs=[hbm] * 5 + [pl.BlockSpec(memory_space=pl.ANY), hbm],
        out_specs=(vmem, vmem),
        scratch_shapes=[
            pltpu.VMEM(brick, jnp.float32),
            pltpu.VMEM(brick, jnp.float32),
            pltpu.VMEM(brick, jnp.float32),
            pltpu.VMEM((size_x, size_y, size_z), jnp.int32),
            pltpu.VMEM(brick, jnp.float32),
            pltpu.VMEM((STEPS,) + brick, jnp.float32),
            pltpu.VMEM((STEPS, 2, size_y // 2, two, size_z), jnp.bfloat16),
            pltpu.VMEM((STEPS + 1, 2, size_y // 2, two, size_z), jnp.bfloat16),
            pltpu.VMEM((STEPS, 2, size_x // 2, two, size_z), jnp.bfloat16),
            pltpu.VMEM((STEPS + 1, 2, size_x // 2, two, size_z), jnp.bfloat16),
            pltpu.VMEM((STEPS, channels, size_z), jnp.float32),
            pltpu.VMEM((STEPS + 1, 2, channels, size_z), jnp.float32),
            pltpu.VMEM((devices, 4, slots), jnp.float32),
            pltpu.VMEM((3, slots, slots), jnp.float32),
            pltpu.VMEM((rows, slots, group * slots), jnp.bfloat16),
            pltpu.VMEM((ROUNDS, channels, slots), jnp.bfloat16),
            pltpu.VMEM((ROUNDS, devices, channels, slots), jnp.bfloat16),
            pltpu.VMEM((size_x * size_y, channels, slots), jnp.float32),
            pltpu.SMEM(class_shift.shape, jnp.float32),
            pltpu.VMEM((1, 1), jnp.int32),
            pltpu.VMEM((1, slots), jnp.int32),
            pltpu.VMEM(panel_geometry.shape, jnp.float32),
            pltpu.SemaphoreType.DMA((7,)),
            pltpu.SemaphoreType.DMA((1,)),
            pltpu.SemaphoreType.DMA((2, 6)),
            pltpu.SemaphoreType.DMA((1,)),
            pltpu.SemaphoreType.DMA((1,)),
            pltpu.SemaphoreType.DMA((ROUNDS, rows)),
        ],
        compiler_params=pltpu.CompilerParams(
            collective_id=0, has_side_effects=True, vmem_limit_bytes=grant
        ),
    )(*operands)
    return pl.pallas_call(
        place,
        out_shape=(
            jax.ShapeDtypeStruct(initial_field.shape, jnp.float32),
            jax.ShapeDtypeStruct((channels, slots), jnp.float32),
        ),
        in_specs=[vmem] * 2,
        out_specs=(hbm, hbm),
        scratch_shapes=[pltpu.SemaphoreType.DMA((2,))],
        compiler_params=pltpu.CompilerParams(vmem_limit_bytes=8 * math.prod(brick)),
    )(field, potential)


def solution(mesh):
    placed = (
        P(None, "row", "col", "gz"),
        P(None, "row", "col", "gz"),
        P("row", "col", "gz"),
        P(),
        P(("row", "col", "gz")),
        P(("row", "col", "gz")),
        P(None, ("row", "col", "gz")),
    )
    return jax.shard_map(
        functools.partial(local, tuple(mesh.shape[axis] for axis in AXES)),
        mesh=mesh,
        in_specs=placed,
        out_specs=(P(None, "row", "col", "gz"), P(None, ("row", "col", "gz"))),
        check_vma=False,
    )
```

time: 37.2 us -> 34.2 us (0.919)
  Pallas kernels: 34.5 us -> 32.7 us
  local copies, waits for them, and re-layouts: 1.3 us -> 0 us
    pallas_call x1, Pallas kernels: 34.5 us -> 32 us  [local(): pl.pallas_call(functools.partial(kernel, sizes), out_shape=(jax.ShapeDtyp...]
    unnamed x2 -> x0, local copies, waits for them, and re-layouts: 1.3 us -> none
    pallas_call x0 -> x1, Pallas kernels: none -> 0.71 us  [local(): pl.pallas_call(place, out_shape=(jax.ShapeDtypeStruct(initial_field.shape...]
where the time goes in v1:
time: 34.2 us; the launch traced here: 34 us
  Pallas kernels  32.7 us (96%)
  between operations  1.29 us (4%)
    pallas_call x1, Pallas kernels, local(): pl.pallas_call(functools.partial(kernel, sizes), out_shape=(jax.ShapeDtyp...  32 us
    pallas_call x1, Pallas kernels, local(): pl.pallas_call(place, out_shape=(jax.ShapeDtypeStruct(initial_field.shape...  0.71 us

profile of v1, /device:TPU:0, one launch (start us, length us, event | category | flops | bytes accessed | tf_op | source)
XLA Modules:
  0.0 34.0 jit_solution(11685037246874893573)
XLA Ops:
  1.3 32.0 %shard_map.86 = (f32[4,16,8,128]{3,2,1,0:T(8,128)S(1)}, f32[8,128]{1,0:T(8,128)S(1)}) custom-call(f32[8,4,16,128]{3,2,1,0:T(8,128)} %init_hbm.1, f32[8,4,16,128]{3,2,1,0:T(8,128)} %source_hbm.1, s32[4,16,128]{2,1,0:T(8,128)} %class_hbm.1, f32[16]{0:T(128)} %shift_hbm.1, s32[1,128]{1,0:T(1,128)} %bitcast.3, s32[1,1]{1,0:T(1,128)} %bitcast.2.live_hbm, ...), custom_call_target="tpu_custom_call" | custom-call | tf_op jit(solution)/shard_map/pallas_call | solution.py:441
  33.3 0.7 %shard_map.87 = (f32[8,4,16,128]{3,2,1,0:T(8,128)}, f32[8,128]{1,0:T(8,128)}) custom-call(f32[4,16,8,128]{3,2,1,0:T(8,128)S(1)} %get-tuple-element.4.field_v, f32[8,128]{1,0:T(8,128)S(1)} %get-tuple-element.5.potential_v), custom_call_target="tpu_custom_call" | custom-call | tf_op jit(solution)/shard_map/pallas_call | solution.py:483

commit v2 on v1

--- a/solution.py
+++ b/solution.py
@@ -9,9 +9,7 @@
 from jax.experimental.pallas import tpu as pltpu
 from jax.sharding import PartitionSpec as P
 
-SWEEPS = 3
 ROUNDS = 2
-STEPS = SWEEPS * ROUNDS
 
 relax_weight = 0.8
 wave_number = 25.0
@@ -47,7 +45,8 @@
     init_hbm, source_hbm, class_hbm, shift_hbm, cell_hbm, live_hbm, geo_hbm,
     field_ref, potential_ref,
     init_v, source_v, forcing_v, class_v, weight_v, state_v,
-    x_out, x_in, y_out, y_in, z_out, z_in,
+    x_out, x_in, y_out, y_in, z_out, z_in, xy_in, xz_in, yz_in,
+    wx_out, wx_in, wy_out, wy_in, wz_out, wz_in, rim_x, rim_y, rim_z,
     geo_all, column_v, tile_v, density_out, density_all, at_cell,
     shift_ref, live_ref, cell_ref, geo_ref,
     local_sem, face_send, face_recv, gather_send, geo_recv, density_recv,
@@ -113,80 +112,169 @@
     cell_shape = (channels, size_z)
     lane = lax.broadcasted_iota(jnp.int32, cell_shape, 1)
     pair = lane >> 1
+    even = (lane & 1) == 0
     edge = (lane == 0) | (lane == size_z - 1)
     slab = (size_y * channels, size_z)
     slab_lane = lax.broadcasted_iota(jnp.int32, slab, 1)
-
-    def pack(k, x, values, packed):
-        if x == 0 or x == size_x - 1:
-            for y in range(0, size_y, 2):
-                both = jnp.concatenate([values[y], values[y + 1]], axis=0).astype(x_out.dtype)
-                if x == 0:
-                    x_out[k, 0, y // 2] = both
-                if x == size_x - 1:
-                    x_out[k, 1, y // 2] = both
-        half = pl.ds(channels * (x % 2), channels)
-        y_out[k, 0, x // 2, half, :] = values[0].astype(y_out.dtype)
-        y_out[k, 1, x // 2, half, :] = values[size_y - 1].astype(y_out.dtype)
-        for y in range(size_y):
-            at = x * size_y + y
-            turned = pltpu.roll(values[y], (2 * at + 1) % size_z, 1)
-            packed = jnp.where(pair == at, turned, packed)
+    first_line = lax.rem(pair, size_y) == 0
+    last_line = lax.rem(pair, size_y) == size_y - 1
+    low_plane, high_plane = pair < size_y, pair >= (size_x - 1) * size_y
+
+    def turn(value, shift):
+        return pltpu.roll(value, shift % size_z, 1)
+
+    def half_of_pair(i):
+        return slice(channels * (i % 2), channels * (i % 2) + channels)
+
+    def pack_flat(q, level, values, depth=1):
+        for step in range(depth):
+            for side, x in ((0, step), (1, size_x - 1 - step)):
+                for y in range(0, size_y, 2):
+                    both = jnp.concatenate([values[x][y], values[x][y + 1]], axis=0)
+                    x_out[q, side, level + step, y // 2] = both.astype(x_out.dtype)
+            for side, y in ((0, step), (1, size_y - 1 - step)):
+                for x in range(0, size_x, 2):
+                    both = jnp.concatenate([values[x][y], values[x + 1][y]], axis=0)
+                    y_out[q, side, level + step, x // 2] = both.astype(y_out.dtype)
+
+    def pack_deep(values, depth=1):
+        packed = [jnp.zeros(cell_shape, jnp.float32)] * depth
+        for x in range(size_x):
+            for y in range(size_y):
+                at, value = x * size_y + y, values[x][y]
+                here_now = pair == at
+                packed[0] = jnp.where(here_now, turn(value, 2 * at + 1), packed[0])
+                if depth == 2:
+                    both = jnp.where(even, turn(value, 2 * at + 2), turn(value, 2 * at))
+                    packed[1] = jnp.where(here_now, both, packed[1])
         return packed
 
-    def face_copies(k):
+    def planes(ref):
+        return [[ref[x, y] for y in range(size_y)] for x in range(size_x)]
+
+    def pack(q, values, depth=1):
+        pack_flat(q, 0, values, depth)
+        for step, packed in enumerate(pack_deep(values, depth)):
+            z_out[q, step] = packed
+
+    def pack_force(q, values):
+        pack_flat(q, 2, values)
+        z_out[q, 2] = pack_deep(values)[0]
+
+    numbers = {}
+
+    def number(*key):
+        return numbers.setdefault(key, len(numbers))
+
+    def sided(axis, side):
+        return 0 if sizes[axis] == 2 else side
+
+    def there(axis, up):
+        return here[axis] + (1 if up else -1)
+
+    def exists(axis, up):
+        return here[axis] < sizes[axis] - 1 if up else here[axis] > 0
+
+    faces = [(axis, up) for axis in range(3) if sizes[axis] > 1 for up in (0, 1)]
+    corners = [
+        (a, ua, b, ub)
+        for a, b in ((0, 1), (0, 2), (1, 2))
+        if sizes[a] > 1 and sizes[b] > 1
+        for ua in (0, 1)
+        for ub in (0, 1)
+    ]
+    outs, ins = (x_out, y_out, z_out), (x_in, y_in, z_in)
+    edge_ins = {(0, 1): xy_in, (0, 2): xz_in, (1, 2): yz_in}
+
+    def exchange(q):
+        double = q % 2
+        span = pl.ds(0, 3 if double else 1)
         made = []
-        for axis, (send, receive) in enumerate(((x_out, x_in), (y_out, y_in), (z_out, z_in))):
-            count = sizes[axis]
-            if count == 1:
-                continue
-            for up in (0, 1):
-                target = {AXES[axis]: here[axis] + (1 if up else -1)}
-                source = send.at[k] if axis == 2 else send.at[k, up]
-                side = 0 if count == 2 else 1 - up
-                copy = functools.partial(
-                    pltpu.make_async_remote_copy,
-                    src_ref=source,
-                    dst_ref=receive.at[k, 1 - up],
-                    send_sem=face_send.at[0],
-                    recv_sem=face_recv.at[k % 2, 2 * axis + side],
-                    device_id=target,
-                    device_id_type=MESH,
-                )
-                landed = receive.at[k, up]
-                got = functools.partial(
-                    pltpu.make_async_copy,
-                    landed,
-                    landed,
-                    face_recv.at[k % 2, 2 * axis + (0 if count == 2 else up)],
-                )
-                exists = here[axis] < count - 1 if up else here[axis] > 0
-                made.append((copy, got, exists))
+
+        def add(source, landing, key_out, key_in, target, present):
+            send = functools.partial(
+                pltpu.make_async_remote_copy,
+                src_ref=source,
+                dst_ref=landing[0],
+                send_sem=face_send.at[0],
+                recv_sem=face_recv.at[number(double, *key_out)],
+                device_id=target,
+                device_id_type=MESH,
+            )
+            wait = functools.partial(
+                pltpu.make_async_copy, landing[1], landing[1], face_recv.at[number(double, *key_in)]
+            )
+            made.append((send, wait, present))
+
+        for axis, up in faces:
+            source = outs[axis].at[q, span] if axis == 2 else outs[axis].at[q, up, span]
+            landing = [ins[axis].at[q, side, span] for side in (1 - up, up)]
+            add(
+                source, landing, (axis, sided(axis, 1 - up)), (axis, sided(axis, up)),
+                {AXES[axis]: there(axis, up)}, exists(axis, up),
+            )
+        for a, ua, b, ub in corners if double else ():
+            if (a, b) == (0, 1):
+                source = y_out.at[q, ub, 0, (size_x - 1) // 2 if ua else 0]
+            else:
+                source = z_out.at[q, 0]
+            into = edge_ins[a, b]
+            landing = [into.at[q // 2, 1 - ua, 1 - ub], into.at[q // 2, ua, ub]]
+            add(
+                source, landing,
+                (a, b, sided(a, 1 - ua), sided(b, 1 - ub)), (a, b, sided(a, ua), sided(b, ub)),
+                {AXES[a]: there(a, ua), AXES[b]: there(b, ub)}, exists(a, ua) & exists(b, ub),
+            )
         return made
 
-    def start_faces(k):
-        for copy, _, exists in face_copies(k):
-            pl.when(exists)(lambda copy=copy: copy().start())
-
-    def await_faces(k):
-        for _, got, exists in face_copies(k):
-            pl.when(exists)(lambda got=got: got().wait())
-
-    def finish_faces(k):
-        for copy, _, exists in face_copies(k):
-            pl.when(exists)(lambda copy=copy: copy().wait_send())
-
-    x_in[STEPS] = jnp.zeros(x_in.shape[1:], x_in.dtype)
-    y_in[STEPS] = jnp.zeros(y_in.shape[1:], y_in.dtype)
-    z_in[STEPS] = jnp.zeros(z_in.shape[1:], z_in.dtype)
+    def weight_messages():
+        made = []
+        for axis, up in faces:
+            send_ref, receive = ((wx_out, wx_in), (wy_out, wy_in), (wz_out, wz_in))[axis]
+            source = send_ref if axis == 2 else send_ref.at[up]
+            send = functools.partial(
+                pltpu.make_async_remote_copy,
+                src_ref=source,
+                dst_ref=receive.at[1 - up],
+                send_sem=face_send.at[0],
+                recv_sem=face_recv.at[number("weight", axis, sided(axis, 1 - up))],
+                device_id={AXES[axis]: there(axis, up)},
+                device_id_type=MESH,
+            )
+            landed = receive.at[up]
+            wait = functools.partial(
+                pltpu.make_async_copy, landed, landed,
+                face_recv.at[number("weight", axis, sided(axis, up))],
+            )
+            made.append((send, wait, exists(axis, up)))
+        return made
+
+    def start(made):
+        for send, _, present in made:
+            pl.when(present)(lambda send=send: send().start())
+
+    def land(made):
+        for _, wait, present in made:
+            pl.when(present)(lambda wait=wait: wait().wait())
+
+    def drain(made):
+        for send, _, present in made:
+            pl.when(present)(lambda send=send: send().wait_send())
+
+    none = 2 * ROUNDS
+    x_in[none] = jnp.zeros(x_in.shape[1:], x_in.dtype)
+    y_in[none] = jnp.zeros(y_in.shape[1:], y_in.dtype)
+    z_in[none] = jnp.zeros(z_in.shape[1:], z_in.dtype)
+    for into in edge_ins.values():
+        into[ROUNDS] = jnp.zeros(into.shape[1:], into.dtype)
+    wx_in[2] = jnp.zeros(wx_in.shape[1:], wx_in.dtype)
+    wy_in[2] = jnp.zeros(wy_in.shape[1:], wy_in.dtype)
+    wz_in[2] = jnp.zeros(wz_in.shape[1:], wz_in.dtype)
 
     with jax.named_scope("w_init"):
         brick_wait(init_v, local_sem.at[0])
 
-    packed = jnp.zeros(cell_shape, jnp.float32)
-    for x in range(size_x):
-        packed = pack(0, x, [init_v[x, y] for y in range(size_y)], packed)
-    z_out[0] = packed
+    pack(0, planes(init_v))
 
     copies[1].wait()
     eye = lax.broadcasted_iota(jnp.int32, (slots, slots), 0) == lax.broadcasted_iota(
@@ -199,7 +287,7 @@
 
     with jax.named_scope("w_barrier"):
         pl.semaphore_wait(barrier, devices - 1)
-    start_faces(0)
+    start(exchange(0))
 
     def start_gather(source, gathered, sem):
         def send(device):
@@ -230,6 +318,14 @@
             shift = jnp.where(kind == level, shift_ref[level], shift)
         weight = relax_weight / (6.0 + shift)
         weight_v[x] = jnp.broadcast_to(weight[:, None, :], (size_y, channels, size_z))
+        if x == 0:
+            wx_out[0] = weight
+        if x == size_x - 1:
+            wx_out[1] = weight
+        wy_out[0, x : x + 1, :] = weight[0:1]
+        wy_out[1, x : x + 1, :] = weight[size_y - 1 : size_y]
+    wz_out[...] = pack_deep(planes(weight_v))[0]
+    start(weight_messages())
 
     copies[3].wait()
     copies[4].wait()
@@ -245,66 +341,145 @@
         )
     live = lax.broadcasted_iota(jnp.int32, (channels, slots), 1) < live_ref[...]
     brick_wait(source_v, local_sem.at[2])
-
-    def now(k, x):
-        return init_v[x] if k == 0 else state_v[k - 1, x]
-
-    def inner(k):
-        force = source_v if k <= SWEEPS else forcing_v
+    for x in range(size_x):
+        forcing_v[0, x] = weight_v[x] * source_v[x]
+    pack_force(1, planes(forcing_v.at[0]))
+
+    def inside(value, above, below, first=None, final=None):
         blank = jnp.zeros((1,) + cell_shape, jnp.float32)
+        first = blank if first is None else first[None]
+        final = blank if final is None else final[None]
+        around = jnp.concatenate([value[1:], final], axis=0)
+        around = around + jnp.concatenate([first, value[:-1]], axis=0)
+        for other in (above, below):
+            if other is not None:
+                around = around + other
+        flat = value.reshape(slab)
+        beside = jnp.where(slab_lane == size_z - 1, 0.0, turn(flat, size_z - 1))
+        beside = beside + jnp.where(slab_lane == 0, 0.0, turn(flat, 1))
+        return around + beside.reshape(value.shape)
+
+    def ends(beyond, at):
+        return jnp.where(edge, turn(beyond, -2 * at), 0.0)
+
+    def inner(source, target, force):
         for x in range(size_x):
-            value = now(k, x)
-            around = force[x]
-            if x + 1 < size_x:
-                around = around + now(k, x + 1)
-            if x > 0:
-                around = around + now(k, x - 1)
-            around = around + jnp.concatenate([value[1:], blank], axis=0)
-            around = around + jnp.concatenate([blank, value[:-1]], axis=0)
-            flat = value.reshape(slab)
-            beside = jnp.where(slab_lane == size_z - 1, 0.0, pltpu.roll(flat, size_z - 1, 1))
-            beside = beside + jnp.where(slab_lane == 0, 0.0, pltpu.roll(flat, 1, 1))
-            around = around + beside.reshape(value.shape)
-            state_v[k, x] = (1.0 - relax_weight) * value + weight_v[x] * around
-
-    def outer(k):
-        last = k == STEPS - 1
-        slot = []
-        for axis in range(3):
-            below = jnp.where(here[axis] > 0, k, STEPS)
-            above = jnp.where(here[axis] < sizes[axis] - 1, k, STEPS)
-            slot.append((below, above))
-        beyond = jnp.where(
-            (lane & 1) == 0, z_in[slot[2][0], 0], pltpu.roll(z_in[slot[2][1], 1], size_z - 2, 1)
+            value = source[x]
+            around = inside(
+                value,
+                source[x + 1] if x + 1 < size_x else None,
+                source[x - 1] if x > 0 else None,
+            )
+            target[x] = (1.0 - relax_weight) * value + force[x] + weight_v[x] * around
+
+    def pick(axis, q):
+        return (
+            jnp.where(here[axis] > 0, q, none),
+            jnp.where(here[axis] < sizes[axis] - 1, q, none),
         )
-        packed = jnp.zeros(cell_shape, jnp.float32)
+
+    def from_x(q, side, level, y):
+        both = x_in[pick(0, q)[side], side, level, y // 2].astype(jnp.float32)
+        return both[half_of_pair(y)]
+
+    def from_y(q, side, level, x):
+        both = y_in[pick(1, q)[side], side, level, x // 2].astype(jnp.float32)
+        return both[half_of_pair(x)]
+
+    def from_z(q, level):
+        below, above = pick(2, q)
+        return jnp.where(even, z_in[below, 0, level], z_in[above, 1, level])
+
+    def beside_ends(natural):
+        return jnp.where(even, natural, turn(natural, -2))
+
+    def corner(a, b, q, side_a, side_b):
+        there_a = here[a] > 0 if side_a == 0 else here[a] < sizes[a] - 1
+        there_b = here[b] > 0 if side_b == 0 else here[b] < sizes[b] - 1
+        return edge_ins[a, b][jnp.where(there_a & there_b, q // 2, ROUNDS), side_a, side_b]
+
+    def corner_xy(q, side_x, side_y):
+        both = corner(0, 1, q, side_x, side_y).astype(jnp.float32)
+        return both[half_of_pair(size_x - 1 if side_x == 0 else 0)]
+
+    def corner_z(axis, q, side):
+        return jnp.where(even, corner(axis, 2, q, side, 0), corner(axis, 2, q, side, 1))
+
+    def outer(target, q):
+        beyond = beside_ends(from_z(q, 0))
         for x in range(size_x):
-            results = []
             for y in range(size_y):
-                at = x * size_y + y
-                around = jnp.where(
-                    edge, pltpu.roll(beyond, (2 * size_z - 2 * at) % size_z, 1), 0.0
+                around = ends(beyond, x * size_y + y)
+                if x == 0:
+                    around = around + from_x(q, 0, 0, y)
+                if x == size_x - 1:
+                    around = around + from_x(q, 1, 0, y)
+                if y == 0:
+                    around = around + from_y(q, 0, 0, x)
+                if y == size_y - 1:
+                    around = around + from_y(q, 1, 0, x)
+                target[x, y] = target[x, y] + weight_v[x, y] * around
+
+    def rim(source, q):
+        for side in (0, 1):
+            x = (size_x - 1) * side
+            value = jnp.stack([from_x(q, side, 0, y) for y in range(size_y)])
+            far = jnp.stack([from_x(q, side, 1, y) for y in range(size_y)])
+            force = jnp.stack([from_x(q, side, 2, y) for y in range(size_y)])
+            across = beside_ends(corner_z(0, q, side))
+            theirs = size_x - 1 - x
+            beyond = jnp.stack([ends(across, theirs * size_y + y) for y in range(size_y)])
+            around = beyond + inside(
+                value, source[x], far, corner_xy(q, side, 0), corner_xy(q, side, 1)
+            )
+            weight = wx_in[jnp.where(exists(0, side), side, 2)]
+            weight = jnp.broadcast_to(weight[:, None, :], value.shape)
+            rim_x[side] = (1.0 - relax_weight) * value + force + weight * around
+        for side in (0, 1):
+            y = (size_y - 1) * side
+            theirs = size_y - 1 - y
+            across = beside_ends(corner_z(1, q, side))
+            values = [from_y(q, side, 0, x) for x in range(size_x)]
+            values = [corner_xy(q, 0, side)] + values + [corner_xy(q, 1, side)]
+            weight = wy_in[jnp.where(exists(1, side), side, 2)]
+            for x in range(size_x):
+                value = values[x + 1]
+                around = values[x] + values[x + 2] + source[x, y] + from_y(q, side, 1, x)
+                around = around + ends(across, x * size_y + theirs)
+                around = around + jnp.where(lane == size_z - 1, 0.0, turn(value, size_z - 1))
+                around = around + jnp.where(lane == 0, 0.0, turn(value, 1))
+                rim_y[side, x] = (
+                    (1.0 - relax_weight) * value
+                    + from_y(q, side, 2, x)
+                    + weight[x : x + 1, :] * around
                 )
-                half = slice(channels * (y % 2), channels * (y % 2 + 1))
-                if x == 0:
-                    around = around + x_in[slot[0][0], 0, y // 2].astype(jnp.float32)[half]
-                if x == size_x - 1:
-                    around = around + x_in[slot[0][1], 1, y // 2].astype(jnp.float32)[half]
-                half = slice(channels * (x % 2), channels * (x % 2 + 1))
-                if y == 0:
-                    around = around + y_in[slot[1][0], 0, x // 2].astype(jnp.float32)[half]
-                if y == size_y - 1:
-                    around = around + y_in[slot[1][1], 1, x // 2].astype(jnp.float32)[half]
-                result = state_v[k, x, y] + weight_v[x, y] * around
-                if last:
-                    field_ref[x, y] = result
-                else:
-                    state_v[k, x, y] = result
-                results.append(result)
-            if not last:
-                packed = pack(k + 1, x, results, packed)
-        if not last:
-            z_out[k + 1] = packed
+        value = from_z(q, 0)
+        own = z_out[q, 0]
+        around = from_z(q, 1) + jnp.where(even, turn(own, -1), turn(own, 1))
+        step = 2 * size_y
+        around = around + turn(jnp.where(high_plane, corner_z(0, q, 0), value), step)
+        around = around + turn(jnp.where(low_plane, corner_z(0, q, 1), value), -step)
+        wrap = 2 * (size_y - 1)
+        around = around + jnp.where(first_line, turn(corner_z(1, q, 0), -wrap), turn(value, 2))
+        around = around + jnp.where(last_line, turn(corner_z(1, q, 1), wrap), turn(value, -2))
+        weight = jnp.where(
+            even, wz_in[jnp.where(exists(2, 0), 0, 2)], wz_in[jnp.where(exists(2, 1), 1, 2)]
+        )
+        rim_z[...] = (1.0 - relax_weight) * value + from_z(q, 2) + weight * around
+
+    def whole(source, target, force):
+        beyond = beside_ends(rim_z[...])
+        for x in range(size_x):
+            value = source[x]
+            around = inside(
+                value,
+                source[x + 1] if x + 1 < size_x else rim_x[1],
+                source[x - 1] if x > 0 else rim_x[0],
+                rim_y[0, x],
+                rim_y[1, x],
+            )
+            around = around + jnp.stack([ends(beyond, x * size_y + y) for y in range(size_y)])
+            target[x] = (1.0 - relax_weight) * value + force[x] + weight_v[x] * around
 
     pieces = 4
     chunk = slots // pieces
@@ -341,47 +516,25 @@
             )
         return total
 
-    for k in range(STEPS):
-        if k != SWEEPS:
-            with jax.named_scope(f"inner{k}"):
-                inner(k)
-        if k == 2:
-            with jax.named_scope("w_geogather"):
-                await_gather(geo_all, devices - 1, geo_recv.at[0])
-            with jax.named_scope("tilesA"):
-                make_tiles(0, rows // 4)
-        with jax.named_scope(f"w_faces{k}"):
-            await_faces(k)
-        with jax.named_scope(f"outer{k}"):
-            outer(k)
-        end = k % SWEEPS == SWEEPS - 1
-        if k + 1 < STEPS:
-            start_faces(k + 1)
-        if not end:
-            continue
-        r = k // SWEEPS
-        with jax.named_scope(f"density{r}"):
-            ending = field_ref if k == STEPS - 1 else state_v.at[k]
-            flat = ending[...].reshape(size_x * size_y * channels, size_z).astype(jnp.bfloat16)
-            picked = jnp.dot(flat, pick_z, preferred_element_type=jnp.float32)
-            picked = picked.reshape(size_x * size_y, channels, slots)
-            density = jnp.sum(picked * at_cell[...], axis=0)
-            density = jnp.where(live, density, 0.0).astype(jnp.bfloat16)
-            density_out[r] = density
-            density_all[r, me] = density
-        with jax.named_scope(f"st_dens{r}"):
-            start_gather(density_out.at[r], density_all.at[r], density_recv.at[r, here[0]])
-        if r < ROUNDS - 1:
-            with jax.named_scope(f"inner{k+1}"):
-                inner(k + 1)
-        if r == 0:
+    for r in range(ROUNDS):
+        single, double = 2 * r, 2 * r + 1
+        before = init_v if r == 0 else state_v.at[2]
+        once, mid, after = state_v.at[0], state_v.at[1], state_v.at[2]
+        if r == ROUNDS - 1:
+            after = field_ref
+        force = forcing_v.at[r]
+        with jax.named_scope(f"inner{r}"):
+            inner(before, once, forcing_v.at[0])
+        if r > 0:
             with jax.named_scope("tilesB"):
                 make_tiles(rows // 4, rows)
-        with jax.named_scope(f"apply{r}"):
-            potential = jnp.where(live, apply_tiles(r), 0.0)
-        if r == ROUNDS - 1:
-            potential_ref[...] = potential
-        else:
+        with jax.named_scope(f"w_single{r}"):
+            land(exchange(single))
+        with jax.named_scope(f"outer{r}"):
+            outer(once, single)
+        if r > 0:
+            with jax.named_scope(f"apply{r-1}"):
+                potential = jnp.where(live, apply_tiles(r - 1), 0.0)
             with jax.named_scope(f"load{r}"):
                 half_of = coupling * potential
                 big = half_of.astype(jnp.bfloat16).astype(jnp.float32)
@@ -394,12 +547,52 @@
                         (((1,), (1,)), ((), ())), preferred_element_type=jnp.float32,
                     )
                 load = load.reshape(size_x, size_y, channels, size_z)
-                forcing_v[...] = source_v[...] + load
-                state_v[k + 1] = state_v[k + 1] + weight_v[...] * load
+                for x in range(size_x):
+                    change = weight_v[x] * load[x]
+                    force[x] = forcing_v[0, x] + change
+                    once[x] = once[x] + change
+                pack_force(double, planes(force))
+        with jax.named_scope(f"pack{r}"):
+            pack(double, planes(once), 2)
+        start(exchange(double))
+        with jax.named_scope(f"innerd{r}"):
+            inner(once, mid, force)
+        if r == 0:
+            with jax.named_scope("w_weights"):
+                land(weight_messages())
+            with jax.named_scope("w_geogather"):
+                await_gather(geo_all, devices - 1, geo_recv.at[0])
+            with jax.named_scope("tilesA"):
+                make_tiles(0, rows // 4)
+        with jax.named_scope(f"w_double{r}"):
+            land(exchange(double))
+        with jax.named_scope(f"outerd{r}"):
+            outer(mid, double)
+        with jax.named_scope(f"rim{r}"):
+            rim(once, double)
+        with jax.named_scope(f"whole{r}"):
+            whole(mid, after, force)
+        if r < ROUNDS - 1:
+            with jax.named_scope(f"pack_s{r}"):
+                pack(2 * r + 2, planes(after))
+            start(exchange(2 * r + 2))
+        with jax.named_scope(f"density{r}"):
+            flat = after[...].reshape(size_x * size_y * channels, size_z).astype(jnp.bfloat16)
+            picked = jnp.dot(flat, pick_z, preferred_element_type=jnp.float32)
+            picked = picked.reshape(size_x * size_y, channels, slots)
+            density = jnp.sum(picked * at_cell[...], axis=0)
+            density = jnp.where(live, density, 0.0).astype(jnp.bfloat16)
+            density_out[r] = density
+            density_all[r, me] = density
+        with jax.named_scope(f"st_dens{r}"):
+            start_gather(density_out.at[r], density_all.at[r], density_recv.at[r, here[0]])
+    with jax.named_scope(f"apply{ROUNDS-1}"):
+        potential_ref[...] = jnp.where(live, apply_tiles(ROUNDS - 1), 0.0)
 
     with jax.named_scope("finish"):
-        for k in range(STEPS):
-            finish_faces(k)
+        for q in range(2 * ROUNDS):
+            drain(exchange(q))
+        drain(weight_messages())
         await_gather(geo_all, devices - 1, gather_send.at[0])
         for r in range(ROUNDS):
             await_gather(density_all.at[r], devices - 1, gather_send.at[0])
@@ -428,7 +621,7 @@
     vmem = pl.BlockSpec(memory_space=pltpu.VMEM)
     hbm = pl.BlockSpec(memory_space=pltpu.HBM)
     per_device = slots * (2 * slots + 4 * 8 + ROUNDS * 2 * 2 * channels)
-    grant = devices * per_device + 24 * 4 * math.prod(brick)
+    grant = devices * per_device + 36 * 4 * math.prod(brick)
     operands = [
         pltpu.with_memory_space_constraint(array, pltpu.HBM)
         for array in (
@@ -437,7 +630,9 @@
         )
     ]
     operands.insert(5, live_count.reshape(1, 1))
-    two = 2 * channels
+    two, turns = 2 * channels, 2 * ROUNDS
+    sides = [min(count, 3) - 1 for count in sizes]
+    crossed = sides[0] * sides[1] + sides[0] * sides[2] + sides[1] * sides[2]
     field, potential = pl.pallas_call(
         functools.partial(kernel, sizes),
         out_shape=(
@@ -449,16 +644,28 @@
         scratch_shapes=[
             pltpu.VMEM(brick, jnp.float32),
             pltpu.VMEM(brick, jnp.float32),
-            pltpu.VMEM(brick, jnp.float32),
+            pltpu.VMEM((ROUNDS,) + brick, jnp.float32),
             pltpu.VMEM((size_x, size_y, size_z), jnp.int32),
             pltpu.VMEM(brick, jnp.float32),
-            pltpu.VMEM((STEPS,) + brick, jnp.float32),
-            pltpu.VMEM((STEPS, 2, size_y // 2, two, size_z), jnp.bfloat16),
-            pltpu.VMEM((STEPS + 1, 2, size_y // 2, two, size_z), jnp.bfloat16),
-            pltpu.VMEM((STEPS, 2, size_x // 2, two, size_z), jnp.bfloat16),
-            pltpu.VMEM((STEPS + 1, 2, size_x // 2, two, size_z), jnp.bfloat16),
-            pltpu.VMEM((STEPS, channels, size_z), jnp.float32),
-            pltpu.VMEM((STEPS + 1, 2, channels, size_z), jnp.float32),
+            pltpu.VMEM((3,) + brick, jnp.float32),
+            pltpu.VMEM((turns, 2, 3, size_y // 2, two, size_z), jnp.bfloat16),
+            pltpu.VMEM((turns + 1, 2, 3, size_y // 2, two, size_z), jnp.bfloat16),
+            pltpu.VMEM((turns, 2, 3, size_x // 2, two, size_z), jnp.bfloat16),
+            pltpu.VMEM((turns + 1, 2, 3, size_x // 2, two, size_z), jnp.bfloat16),
+            pltpu.VMEM((turns, 3, channels, size_z), jnp.float32),
+            pltpu.VMEM((turns + 1, 2, 3, channels, size_z), jnp.float32),
+            pltpu.VMEM((ROUNDS + 1, 2, 2, two, size_z), jnp.bfloat16),
+            pltpu.VMEM((ROUNDS + 1, 2, 2, channels, size_z), jnp.float32),
+            pltpu.VMEM((ROUNDS + 1, 2, 2, channels, size_z), jnp.float32),
+            pltpu.VMEM((2, size_y, size_z), jnp.float32),
+            pltpu.VMEM((3, size_y, size_z), jnp.float32),
+            pltpu.VMEM((2, size_x, size_z), jnp.float32),
+            pltpu.VMEM((3, size_x, size_z), jnp.float32),
+            pltpu.VMEM((channels, size_z), jnp.float32),
+            pltpu.VMEM((3, channels, size_z), jnp.float32),
+            pltpu.VMEM((2, size_y, channels, size_z), jnp.float32),
+            pltpu.VMEM((2, size_x, channels, size_z), jnp.float32),
+            pltpu.VMEM((channels, size_z), jnp.float32),
             pltpu.VMEM((devices, 4, slots), jnp.float32),
             pltpu.VMEM((3, slots, slots), jnp.float32),
             pltpu.VMEM((rows, slots, group * slots), jnp.bfloat16),
@@ -471,7 +678,7 @@
             pltpu.VMEM(panel_geometry.shape, jnp.float32),
             pltpu.SemaphoreType.DMA((7,)),
             pltpu.SemaphoreType.DMA((1,)),
-            pltpu.SemaphoreType.DMA((2, 6)),
+            pltpu.SemaphoreType.DMA((3 * sum(sides) + crossed,)),
             pltpu.SemaphoreType.DMA((1,)),
             pltpu.SemaphoreType.DMA((1,)),
             pltpu.SemaphoreType.DMA((ROUNDS, rows)),

time: 34.2 us -> 31.3 us (0.915)
  Pallas kernels: 32.7 us -> 29.8 us
    pallas_call x1, Pallas kernels: 32 us -> 29.1 us  [local(): pl.pallas_call(functools.partial(kernel, sizes), out_shape=(jax.ShapeDtyp...]
where the time goes in v2:
time: 31.3 us; the launch traced here: 31.1 us
  Pallas kernels  29.8 us (95%)
  between operations  1.29 us (4%)
    pallas_call x1, Pallas kernels, local(): pl.pallas_call(functools.partial(kernel, sizes), out_shape=(jax.ShapeDtyp...  29.1 us
    pallas_call x1, Pallas kernels, local(): pl.pallas_call(place, out_shape=(jax.ShapeDtypeStruct(initial_field.shape...  0.71 us

profile of v2, /device:TPU:0, one launch (start us, length us, event | category | flops | bytes accessed | tf_op | source)
XLA Modules:
  0.0 31.1 jit_solution(12034404539512709952)
XLA Ops:
  1.3 29.1 %shard_map.86 = (f32[4,16,8,128]{3,2,1,0:T(8,128)S(1)}, f32[8,128]{1,0:T(8,128)S(1)}) custom-call(f32[8,4,16,128]{3,2,1,0:T(8,128)} %init_hbm.1, f32[8,4,16,128]{3,2,1,0:T(8,128)} %source_hbm.1, s32[4,16,128]{2,1,0:T(8,128)} %class_hbm.1, f32[16]{0:T(128)} %shift_hbm.1, s32[1,128]{1,0:T(1,128)} %bitcast.3, s32[1,1]{1,0:T(1,128)} %bitcast.2.live_hbm, ...), custom_call_target="tpu_custom_call" | custom-call | tf_op jit(solution)/shard_map/pallas_call | solution.py:636
  30.4 0.7 %shard_map.87 = (f32[8,4,16,128]{3,2,1,0:T(8,128)}, f32[8,128]{1,0:T(8,128)}) custom-call(f32[4,16,8,128]{3,2,1,0:T(8,128)S(1)} %get-tuple-element.4.field_v, f32[8,128]{1,0:T(8,128)S(1)} %get-tuple-element.5.potential_v), custom_call_target="tpu_custom_call" | custom-call | tf_op jit(solution)/shard_map/pallas_call | solution.py:690

commit v3 on v2

--- a/solution.py
+++ b/solution.py
@@ -40,6 +40,14 @@
     return value
 
 
+def known_stages(rows):
+    stages, reach = [], max(1, rows // 4)
+    while reach < rows - 1:
+        stages.append(reach)
+        reach *= 2
+    return stages
+
+
 def kernel(
     sizes,
     init_hbm, source_hbm, class_hbm, shift_hbm, cell_hbm, live_hbm, geo_hbm,
@@ -47,9 +55,10 @@
     init_v, source_v, forcing_v, class_v, weight_v, state_v,
     x_out, x_in, y_out, y_in, z_out, z_in, xy_in, xz_in, yz_in,
     wx_out, wx_in, wy_out, wy_in, wz_out, wz_in, rim_x, rim_y, rim_z,
+    rim_wx, rim_wy, rim_wz,
     geo_all, column_v, tile_v, density_out, density_all, at_cell,
     shift_ref, live_ref, cell_ref, geo_ref,
-    local_sem, face_send, face_recv, gather_send, geo_recv, density_recv,
+    known, local_sem, face_send, face_recv, gather_send, geo_recv, density_recv,
 ):
     rows, cols, depths = sizes
     devices = rows * cols * depths
@@ -60,6 +69,45 @@
     factor = 1.0 / math.sqrt(slots * devices)
     here = tuple(lax.axis_index(axis) for axis in AXES)
     me = (here[0] * cols + here[1]) * depths + here[2]
+
+    reach = max(1, rows // 4)
+    barrier = pltpu.get_barrier_semaphore()
+
+    def greet(row, first):
+        for b in range(cols):
+            for c in range(depths):
+                if first and b == 0 and c == 0:
+                    continue
+                pl.semaphore_signal(
+                    barrier, inc=1, device_id_type=MESH,
+                    device_id=(row, lax.rem(here[1] + b, cols), lax.rem(here[2] + c, depths)),
+                )
+
+    greet(here[0], True)
+    for away in range(1, reach + 1):
+        pl.when(here[0] >= away)(lambda: greet(here[0] - away, False))
+        pl.when(here[0] + away < rows)(lambda: greet(here[0] + away, False))
+    near_low = jnp.where(here[0] > reach, here[0] - reach, 0)
+    near_high = jnp.where(here[0] + reach < rows, here[0] + reach, rows - 1)
+    near = (near_high - near_low + 1) * group - 1
+
+    stages = known_stages(rows)
+
+    def pass_on(stage):
+        d = stages[stage]
+
+        def tell(row):
+            pl.semaphore_signal(
+                known.at[stage], inc=1, device_id={"row": row}, device_id_type=MESH
+            )
+
+        pl.when((here[0] >= d) & (here[0] < rows - 1))(lambda: tell(here[0] - d))
+        pl.when((here[0] + d < rows) & (here[0] > 0))(lambda: tell(here[0] + d))
+
+    def hear(stage):
+        d = stages[stage]
+        told = jnp.where(here[0] + d < rows - 1, 1, 0) + jnp.where(here[0] > d, 1, 0)
+        pl.when(told > 0)(lambda: pl.semaphore_wait(known.at[stage], told))
 
     def brick_copies(hbm, vmem, sem):
         return [
@@ -102,10 +150,6 @@
         lax.fori_loop(0, rows - 1, others, 0)
         at(here[0], True)
 
-    barrier = pltpu.get_barrier_semaphore()
-    each_other(
-        lambda device: pl.semaphore_signal(barrier, inc=1, device_id=device, device_id_type=MESH)
-    )
     for copy in brick_copies(source_hbm, source_v, local_sem.at[2]):
         copy.start()
 
@@ -126,40 +170,27 @@
     def half_of_pair(i):
         return slice(channels * (i % 2), channels * (i % 2) + channels)
 
-    def pack_flat(q, level, values, depth=1):
-        for step in range(depth):
-            for side, x in ((0, step), (1, size_x - 1 - step)):
-                for y in range(0, size_y, 2):
-                    both = jnp.concatenate([values[x][y], values[x][y + 1]], axis=0)
-                    x_out[q, side, level + step, y // 2] = both.astype(x_out.dtype)
-            for side, y in ((0, step), (1, size_y - 1 - step)):
-                for x in range(0, size_x, 2):
-                    both = jnp.concatenate([values[x][y], values[x + 1][y]], axis=0)
-                    y_out[q, side, level + step, x // 2] = both.astype(y_out.dtype)
-
-    def pack_deep(values, depth=1):
-        packed = [jnp.zeros(cell_shape, jnp.float32)] * depth
+    def pack_deep(values):
+        packed = jnp.zeros(cell_shape, jnp.float32)
         for x in range(size_x):
             for y in range(size_y):
-                at, value = x * size_y + y, values[x][y]
-                here_now = pair == at
-                packed[0] = jnp.where(here_now, turn(value, 2 * at + 1), packed[0])
-                if depth == 2:
-                    both = jnp.where(even, turn(value, 2 * at + 2), turn(value, 2 * at))
-                    packed[1] = jnp.where(here_now, both, packed[1])
+                at = x * size_y + y
+                packed = jnp.where(pair == at, turn(values[x][y], 2 * at + 1), packed)
         return packed
 
     def planes(ref):
         return [[ref[x, y] for y in range(size_y)] for x in range(size_x)]
 
-    def pack(q, values, depth=1):
-        pack_flat(q, 0, values, depth)
-        for step, packed in enumerate(pack_deep(values, depth)):
-            z_out[q, step] = packed
-
-    def pack_force(q, values):
-        pack_flat(q, 2, values)
-        z_out[q, 2] = pack_deep(values)[0]
+    def pack(q, values):
+        for side, x in ((0, 0), (1, size_x - 1)):
+            for y in range(0, size_y, 2):
+                both = jnp.concatenate([values[x][y], values[x][y + 1]], axis=0)
+                x_out[q, side, y // 2] = both.astype(x_out.dtype)
+        for side, y in ((0, 0), (1, size_y - 1)):
+            for x in range(0, size_x, 2):
+                both = jnp.concatenate([values[x][y], values[x + 1][y]], axis=0)
+                y_out[q, side, x // 2] = both.astype(y_out.dtype)
+        z_out[q] = pack_deep(values)
 
     numbers = {}
 
@@ -186,9 +217,8 @@
     outs, ins = (x_out, y_out, z_out), (x_in, y_in, z_in)
     edge_ins = {(0, 1): xy_in, (0, 2): xz_in, (1, 2): yz_in}
 
-    def exchange(q):
-        double = q % 2
-        span = pl.ds(0, 3 if double else 1)
+    def exchange(q, edges=False):
+        kind = q % 3
         made = []
 
         def add(source, landing, key_out, key_in, target, present):
@@ -197,29 +227,29 @@
                 src_ref=source,
                 dst_ref=landing[0],
                 send_sem=face_send.at[0],
-                recv_sem=face_recv.at[number(double, *key_out)],
+                recv_sem=face_recv.at[number(kind, *key_out)],
                 device_id=target,
                 device_id_type=MESH,
             )
             wait = functools.partial(
-                pltpu.make_async_copy, landing[1], landing[1], face_recv.at[number(double, *key_in)]
+                pltpu.make_async_copy, landing[1], landing[1], face_recv.at[number(kind, *key_in)]
             )
             made.append((send, wait, present))
 
-        for axis, up in faces:
-            source = outs[axis].at[q, span] if axis == 2 else outs[axis].at[q, up, span]
-            landing = [ins[axis].at[q, side, span] for side in (1 - up, up)]
+        for axis, up in () if edges else faces:
+            source = outs[axis].at[q] if axis == 2 else outs[axis].at[q, up]
+            landing = [ins[axis].at[q, side] for side in (1 - up, up)]
             add(
                 source, landing, (axis, sided(axis, 1 - up)), (axis, sided(axis, up)),
                 {AXES[axis]: there(axis, up)}, exists(axis, up),
             )
-        for a, ua, b, ub in corners if double else ():
+        for a, ua, b, ub in corners if edges else ():
             if (a, b) == (0, 1):
-                source = y_out.at[q, ub, 0, (size_x - 1) // 2 if ua else 0]
+                source = y_out.at[q, ub, (size_x - 1) // 2 if ua else 0]
             else:
-                source = z_out.at[q, 0]
+                source = z_out.at[q]
             into = edge_ins[a, b]
-            landing = [into.at[q // 2, 1 - ua, 1 - ub], into.at[q // 2, ua, ub]]
+            landing = [into.at[q // 3, 1 - ua, 1 - ub], into.at[q // 3, ua, ub]]
             add(
                 source, landing,
                 (a, b, sided(a, 1 - ua), sided(b, 1 - ub)), (a, b, sided(a, ua), sided(b, ub)),
@@ -261,7 +291,7 @@
         for send, _, present in made:
             pl.when(present)(lambda send=send: send().wait_send())
 
-    none = 2 * ROUNDS
+    none = 3 * ROUNDS
     x_in[none] = jnp.zeros(x_in.shape[1:], x_in.dtype)
     y_in[none] = jnp.zeros(y_in.shape[1:], y_in.dtype)
     z_in[none] = jnp.zeros(z_in.shape[1:], z_in.dtype)
@@ -286,7 +316,9 @@
     geo_all[me] = geo_ref[...]
 
     with jax.named_scope("w_barrier"):
-        pl.semaphore_wait(barrier, devices - 1)
+        pl.semaphore_wait(barrier, near)
+    if stages:
+        pass_on(0)
     start(exchange(0))
 
     def start_gather(source, gathered, sem):
@@ -305,9 +337,6 @@
     def await_gather(gathered, count, sem):
         whole = gathered.at[pl.ds(0, count)]
         pltpu.make_async_copy(whole, whole, sem).wait()
-
-    with jax.named_scope("st_geo"):
-        start_gather(geo_ref, geo_all, geo_recv.at[0])
 
     copies[0].wait()
     copies[2].wait()
@@ -324,7 +353,7 @@
             wx_out[1] = weight
         wy_out[0, x : x + 1, :] = weight[0:1]
         wy_out[1, x : x + 1, :] = weight[size_y - 1 : size_y]
-    wz_out[...] = pack_deep(planes(weight_v))[0]
+    wz_out[...] = pack_deep(planes(weight_v))
     start(weight_messages())
 
     copies[3].wait()
@@ -343,14 +372,11 @@
     brick_wait(source_v, local_sem.at[2])
     for x in range(size_x):
         forcing_v[0, x] = weight_v[x] * source_v[x]
-    pack_force(1, planes(forcing_v.at[0]))
-
-    def inside(value, above, below, first=None, final=None):
+
+    def inside(value, above, below):
         blank = jnp.zeros((1,) + cell_shape, jnp.float32)
-        first = blank if first is None else first[None]
-        final = blank if final is None else final[None]
-        around = jnp.concatenate([value[1:], final], axis=0)
-        around = around + jnp.concatenate([first, value[:-1]], axis=0)
+        around = jnp.concatenate([value[1:], blank], axis=0)
+        around = around + jnp.concatenate([blank, value[:-1]], axis=0)
         for other in (above, below):
             if other is not None:
                 around = around + other
@@ -378,17 +404,17 @@
             jnp.where(here[axis] < sizes[axis] - 1, q, none),
         )
 
-    def from_x(q, side, level, y):
-        both = x_in[pick(0, q)[side], side, level, y // 2].astype(jnp.float32)
+    def from_x(q, side, y):
+        both = x_in[pick(0, q)[side], side, y // 2].astype(jnp.float32)
         return both[half_of_pair(y)]
 
-    def from_y(q, side, level, x):
-        both = y_in[pick(1, q)[side], side, level, x // 2].astype(jnp.float32)
+    def from_y(q, side, x):
+        both = y_in[pick(1, q)[side], side, x // 2].astype(jnp.float32)
         return both[half_of_pair(x)]
 
-    def from_z(q, level):
+    def from_z(q):
         below, above = pick(2, q)
-        return jnp.where(even, z_in[below, 0, level], z_in[above, 1, level])
+        return jnp.where(even, z_in[below, 0], z_in[above, 1])
 
     def beside_ends(natural):
         return jnp.where(even, natural, turn(natural, -2))
@@ -396,7 +422,7 @@
     def corner(a, b, q, side_a, side_b):
         there_a = here[a] > 0 if side_a == 0 else here[a] < sizes[a] - 1
         there_b = here[b] > 0 if side_b == 0 else here[b] < sizes[b] - 1
-        return edge_ins[a, b][jnp.where(there_a & there_b, q // 2, ROUNDS), side_a, side_b]
+        return edge_ins[a, b][jnp.where(there_a & there_b, q // 3, ROUNDS), side_a, side_b]
 
     def corner_xy(q, side_x, side_y):
         both = corner(0, 1, q, side_x, side_y).astype(jnp.float32)
@@ -406,80 +432,80 @@
         return jnp.where(even, corner(axis, 2, q, side, 0), corner(axis, 2, q, side, 1))
 
     def outer(target, q):
-        beyond = beside_ends(from_z(q, 0))
+        beyond = beside_ends(from_z(q))
         for x in range(size_x):
             for y in range(size_y):
                 around = ends(beyond, x * size_y + y)
                 if x == 0:
-                    around = around + from_x(q, 0, 0, y)
+                    around = around + from_x(q, 0, y)
                 if x == size_x - 1:
-                    around = around + from_x(q, 1, 0, y)
+                    around = around + from_x(q, 1, y)
                 if y == 0:
-                    around = around + from_y(q, 0, 0, x)
+                    around = around + from_y(q, 0, x)
                 if y == size_y - 1:
-                    around = around + from_y(q, 1, 0, x)
+                    around = around + from_y(q, 1, x)
                 target[x, y] = target[x, y] + weight_v[x, y] * around
 
-    def rim(source, q):
+    def spread_weights():
         for side in (0, 1):
-            x = (size_x - 1) * side
-            value = jnp.stack([from_x(q, side, 0, y) for y in range(size_y)])
-            far = jnp.stack([from_x(q, side, 1, y) for y in range(size_y)])
-            force = jnp.stack([from_x(q, side, 2, y) for y in range(size_y)])
-            across = beside_ends(corner_z(0, q, side))
-            theirs = size_x - 1 - x
-            beyond = jnp.stack([ends(across, theirs * size_y + y) for y in range(size_y)])
-            around = beyond + inside(
-                value, source[x], far, corner_xy(q, side, 0), corner_xy(q, side, 1)
-            )
             weight = wx_in[jnp.where(exists(0, side), side, 2)]
-            weight = jnp.broadcast_to(weight[:, None, :], value.shape)
-            rim_x[side] = (1.0 - relax_weight) * value + force + weight * around
-        for side in (0, 1):
-            y = (size_y - 1) * side
-            theirs = size_y - 1 - y
-            across = beside_ends(corner_z(1, q, side))
-            values = [from_y(q, side, 0, x) for x in range(size_x)]
-            values = [corner_xy(q, 0, side)] + values + [corner_xy(q, 1, side)]
+            rim_wx[side] = jnp.broadcast_to(weight[:, None, :], (size_y,) + cell_shape)
             weight = wy_in[jnp.where(exists(1, side), side, 2)]
-            for x in range(size_x):
-                value = values[x + 1]
-                around = values[x] + values[x + 2] + source[x, y] + from_y(q, side, 1, x)
-                around = around + ends(across, x * size_y + theirs)
-                around = around + jnp.where(lane == size_z - 1, 0.0, turn(value, size_z - 1))
-                around = around + jnp.where(lane == 0, 0.0, turn(value, 1))
-                rim_y[side, x] = (
-                    (1.0 - relax_weight) * value
-                    + from_y(q, side, 2, x)
-                    + weight[x : x + 1, :] * around
-                )
-        value = from_z(q, 0)
-        own = z_out[q, 0]
-        around = from_z(q, 1) + jnp.where(even, turn(own, -1), turn(own, 1))
-        step = 2 * size_y
-        around = around + turn(jnp.where(high_plane, corner_z(0, q, 0), value), step)
-        around = around + turn(jnp.where(low_plane, corner_z(0, q, 1), value), -step)
-        wrap = 2 * (size_y - 1)
-        around = around + jnp.where(first_line, turn(corner_z(1, q, 0), -wrap), turn(value, 2))
-        around = around + jnp.where(last_line, turn(corner_z(1, q, 1), wrap), turn(value, -2))
-        weight = jnp.where(
+            rim_wy[side] = jnp.broadcast_to(weight[:, None, :], (size_x,) + cell_shape)
+        rim_wz[...] = jnp.where(
             even, wz_in[jnp.where(exists(2, 0), 0, 2)], wz_in[jnp.where(exists(2, 1), 1, 2)]
         )
-        rim_z[...] = (1.0 - relax_weight) * value + from_z(q, 2) + weight * around
-
-    def whole(source, target, force):
-        beyond = beside_ends(rim_z[...])
+
+    def own_rim(source, q):
+        for side in (0, 1):
+            rim_x[side] = rim_wx[side] * source[(size_x - 1) * side]
+            for x in range(size_x):
+                rim_y[side, x] = rim_wy[side, x] * source[x, (size_y - 1) * side]
+        own = z_out[q]
+        rim_z[...] = rim_wz[...] * jnp.where(even, turn(own, -1), turn(own, 1))
+
+    def edge_rim(q):
+        for side in (0, 1):
+            across = beside_ends(corner_z(0, q, side))
+            theirs = (size_x - 1) * (1 - side)
+            for y in range(size_y):
+                around = ends(across, theirs * size_y + y)
+                if y == 0:
+                    around = around + corner_xy(q, side, 0)
+                if y == size_y - 1:
+                    around = around + corner_xy(q, side, 1)
+                rim_x[side, y] = rim_x[side, y] + rim_wx[side, y] * around
+        for side in (0, 1):
+            across = beside_ends(corner_z(1, q, side))
+            theirs = (size_y - 1) * (1 - side)
+            for x in range(size_x):
+                around = ends(across, x * size_y + theirs)
+                if x == 0:
+                    around = around + corner_xy(q, 0, side)
+                if x == size_x - 1:
+                    around = around + corner_xy(q, 1, side)
+                rim_y[side, x] = rim_y[side, x] + rim_wy[side, x] * around
+        step, wrap = 2 * size_y, 2 * (size_y - 1)
+        around = turn(jnp.where(high_plane, corner_z(0, q, 0), 0.0), step)
+        around = around + turn(jnp.where(low_plane, corner_z(0, q, 1), 0.0), -step)
+        around = around + jnp.where(first_line, turn(corner_z(1, q, 0), -wrap), 0.0)
+        around = around + jnp.where(last_line, turn(corner_z(1, q, 1), wrap), 0.0)
+        rim_z[...] = rim_z[...] + rim_wz[...] * around
+
+    def add_rim(target, q):
+        beyond = beside_ends(rim_z[...] + from_z(q))
         for x in range(size_x):
-            value = source[x]
-            around = inside(
-                value,
-                source[x + 1] if x + 1 < size_x else rim_x[1],
-                source[x - 1] if x > 0 else rim_x[0],
-                rim_y[0, x],
-                rim_y[1, x],
-            )
-            around = around + jnp.stack([ends(beyond, x * size_y + y) for y in range(size_y)])
-            target[x] = (1.0 - relax_weight) * value + force[x] + weight_v[x] * around
+            for y in range(size_y):
+                around = ends(beyond, x * size_y + y)
+                if x == 0:
+                    around = around + (rim_x[0, y] + from_x(q, 0, y))
+                if x == size_x - 1:
+                    around = around + (rim_x[1, y] + from_x(q, 1, y))
+                if y == 0:
+                    around = around + (rim_y[0, x] + from_y(q, 0, x))
+                if y == size_y - 1:
+                    around = around + (rim_y[1, x] + from_y(q, 1, x))
+                target[x, y] = target[x, y] + weight_v[x, y] * around
 
     pieces = 4
     chunk = slots // pieces
@@ -516,8 +542,18 @@
             )
         return total
 
+    def drain_now():
+        for q in range(3 * ROUNDS - 2):
+            drain(exchange(q))
+            if q % 3 == 1:
+                drain(exchange(q, edges=True))
+        drain(weight_messages())
+        await_gather(geo_all, devices - 1, gather_send.at[0])
+        for r in range(ROUNDS - 1):
+            await_gather(density_all.at[r], devices - 1, gather_send.at[0])
+
     for r in range(ROUNDS):
-        single, double = 2 * r, 2 * r + 1
+        single, double = 3 * r, 3 * r + 1
         before = init_v if r == 0 else state_v.at[2]
         once, mid, after = state_v.at[0], state_v.at[1], state_v.at[2]
         if r == ROUNDS - 1:
@@ -527,7 +563,13 @@
             inner(before, once, forcing_v.at[0])
         if r > 0:
             with jax.named_scope("tilesB"):
-                make_tiles(rows // 4, rows)
+                await_gather(geo_all, devices - 1, geo_recv.at[0])
+                make_tiles(0, rows)
+        if r == 0:
+            with jax.named_scope("w_known0"):
+                for stage in range(len(stages) - 1):
+                    hear(stage)
+                    pass_on(stage + 1)
         with jax.named_scope(f"w_single{r}"):
             land(exchange(single))
         with jax.named_scope(f"outer{r}"):
@@ -551,31 +593,40 @@
                     change = weight_v[x] * load[x]
                     force[x] = forcing_v[0, x] + change
                     once[x] = once[x] + change
-                pack_force(double, planes(force))
         with jax.named_scope(f"pack{r}"):
-            pack(double, planes(once), 2)
+            pack(double, planes(once))
+        start(exchange(double, edges=True))
         start(exchange(double))
         with jax.named_scope(f"innerd{r}"):
             inner(once, mid, force)
+        with jax.named_scope(f"packd{r}"):
+            pack(double + 1, planes(mid))
+        start(exchange(double + 1))
         if r == 0:
             with jax.named_scope("w_weights"):
                 land(weight_messages())
-            with jax.named_scope("w_geogather"):
-                await_gather(geo_all, devices - 1, geo_recv.at[0])
-            with jax.named_scope("tilesA"):
-                make_tiles(0, rows // 4)
+                spread_weights()
+            with jax.named_scope("w_known"):
+                if stages:
+                    hear(len(stages) - 1)
+            with jax.named_scope("st_geo"):
+                start_gather(geo_ref, geo_all, geo_recv.at[0])
+        else:
+            drain_now()
+        own_rim(once, double)
         with jax.named_scope(f"w_double{r}"):
             land(exchange(double))
         with jax.named_scope(f"outerd{r}"):
             outer(mid, double)
+            inner(mid, after, force)
+        with jax.named_scope(f"w_edges{r}"):
+            land(exchange(double, edges=True))
+        with jax.named_scope(f"before_rim{r}"):
+            edge_rim(double)
+        with jax.named_scope(f"w_rim{r}"):
+            land(exchange(double + 1))
         with jax.named_scope(f"rim{r}"):
-            rim(once, double)
-        with jax.named_scope(f"whole{r}"):
-            whole(mid, after, force)
-        if r < ROUNDS - 1:
-            with jax.named_scope(f"pack_s{r}"):
-                pack(2 * r + 2, planes(after))
-            start(exchange(2 * r + 2))
+            add_rim(after, double + 1)
         with jax.named_scope(f"density{r}"):
             flat = after[...].reshape(size_x * size_y * channels, size_z).astype(jnp.bfloat16)
             picked = jnp.dot(flat, pick_z, preferred_element_type=jnp.float32)
@@ -586,16 +637,18 @@
             density_all[r, me] = density
         with jax.named_scope(f"st_dens{r}"):
             start_gather(density_out.at[r], density_all.at[r], density_recv.at[r, here[0]])
+        if r < ROUNDS - 1:
+            with jax.named_scope(f"pack_s{r}"):
+                pack(single + 3, planes(after))
+            start(exchange(single + 3))
+    drain(exchange(3 * ROUNDS - 2))
+    drain(exchange(3 * ROUNDS - 2, edges=True))
+    drain(exchange(3 * ROUNDS - 1))
     with jax.named_scope(f"apply{ROUNDS-1}"):
         potential_ref[...] = jnp.where(live, apply_tiles(ROUNDS - 1), 0.0)
 
     with jax.named_scope("finish"):
-        for q in range(2 * ROUNDS):
-            drain(exchange(q))
-        drain(weight_messages())
-        await_gather(geo_all, devices - 1, gather_send.at[0])
-        for r in range(ROUNDS):
-            await_gather(density_all.at[r], devices - 1, gather_send.at[0])
+        await_gather(density_all.at[ROUNDS - 1], devices - 1, gather_send.at[0])
 
 
 def place(field_v, potential_v, field_hbm, potential_hbm, sem):
@@ -630,7 +683,7 @@
         )
     ]
     operands.insert(5, live_count.reshape(1, 1))
-    two, turns = 2 * channels, 2 * ROUNDS
+    two, turns = 2 * channels, 3 * ROUNDS
     sides = [min(count, 3) - 1 for count in sizes]
     crossed = sides[0] * sides[1] + sides[0] * sides[2] + sides[1] * sides[2]
     field, potential = pl.pallas_call(
@@ -648,12 +701,12 @@
             pltpu.VMEM((size_x, size_y, size_z), jnp.int32),
             pltpu.VMEM(brick, jnp.float32),
             pltpu.VMEM((3,) + brick, jnp.float32),
-            pltpu.VMEM((turns, 2, 3, size_y // 2, two, size_z), jnp.bfloat16),
-            pltpu.VMEM((turns + 1, 2, 3, size_y // 2, two, size_z), jnp.bfloat16),
-            pltpu.VMEM((turns, 2, 3, size_x // 2, two, size_z), jnp.bfloat16),
-            pltpu.VMEM((turns + 1, 2, 3, size_x // 2, two, size_z), jnp.bfloat16),
-            pltpu.VMEM((turns, 3, channels, size_z), jnp.float32),
-            pltpu.VMEM((turns + 1, 2, 3, channels, size_z), jnp.float32),
+            pltpu.VMEM((turns, 2, size_y // 2, two, size_z), jnp.bfloat16),
+            pltpu.VMEM((turns + 1, 2, size_y // 2, two, size_z), jnp.bfloat16),
+            pltpu.VMEM((turns, 2, size_x // 2, two, size_z), jnp.bfloat16),
+            pltpu.VMEM((turns + 1, 2, size_x // 2, two, size_z), jnp.bfloat16),
+            pltpu.VMEM((turns, channels, size_z), jnp.float32),
+            pltpu.VMEM((turns + 1, 2, channels, size_z), jnp.float32),
             pltpu.VMEM((ROUNDS + 1, 2, 2, two, size_z), jnp.bfloat16),
             pltpu.VMEM((ROUNDS + 1, 2, 2, channels, size_z), jnp.float32),
             pltpu.VMEM((ROUNDS + 1, 2, 2, channels, size_z), jnp.float32),
@@ -663,6 +716,9 @@
             pltpu.VMEM((3, size_x, size_z), jnp.float32),
             pltpu.VMEM((channels, size_z), jnp.float32),
             pltpu.VMEM((3, channels, size_z), jnp.float32),
+            pltpu.VMEM((2, size_y, channels, size_z), jnp.float32),
+            pltpu.VMEM((2, size_x, channels, size_z), jnp.float32),
+            pltpu.VMEM((channels, size_z), jnp.float32),
             pltpu.VMEM((2, size_y, channels, size_z), jnp.float32),
             pltpu.VMEM((2, size_x, channels, size_z), jnp.float32),
             pltpu.VMEM((channels, size_z), jnp.float32),
@@ -676,9 +732,10 @@
             pltpu.VMEM((1, 1), jnp.int32),
             pltpu.VMEM((1, slots), jnp.int32),
             pltpu.VMEM(panel_geometry.shape, jnp.float32),
+            pltpu.SemaphoreType.REGULAR((max(1, len(known_stages(rows))),)),
             pltpu.SemaphoreType.DMA((7,)),
             pltpu.SemaphoreType.DMA((1,)),
-            pltpu.SemaphoreType.DMA((3 * sum(sides) + crossed,)),
+            pltpu.SemaphoreType.DMA((4 * sum(sides) + crossed,)),
             pltpu.SemaphoreType.DMA((1,)),
             pltpu.SemaphoreType.DMA((1,)),
             pltpu.SemaphoreType.DMA((ROUNDS, rows)),

time: 31.3 us -> 28.7 us (0.917)
  Pallas kernels: 29.8 us -> 27.3 us
    pallas_call x1, Pallas kernels: 29.1 us -> 26.5 us  [local(): pl.pallas_call(functools.partial(kernel, sizes), out_shape=(jax.ShapeDtyp...]
where the time goes in v3:
time: 28.7 us; the launch traced here: 28.5 us
  Pallas kernels  27.3 us (95%)
  between operations  1.29 us (4%)
    pallas_call x1, Pallas kernels, local(): pl.pallas_call(functools.partial(kernel, sizes), out_shape=(jax.ShapeDtyp...  26.5 us
    pallas_call x1, Pallas kernels, local(): pl.pallas_call(place, out_shape=(jax.ShapeDtypeStruct(initial_field.shape...  0.71 us

profile of v3, /device:TPU:0, one launch (start us, length us, event | category | flops | bytes accessed | tf_op | source)
XLA Modules:
  0.0 28.5 jit_solution(3068664633677204705)
XLA Ops:
  1.3 26.5 %shard_map.86 = (f32[4,16,8,128]{3,2,1,0:T(8,128)S(1)}, f32[8,128]{1,0:T(8,128)S(1)}) custom-call(f32[8,4,16,128]{3,2,1,0:T(8,128)} %init_hbm.1, f32[8,4,16,128]{3,2,1,0:T(8,128)} %source_hbm.1, s32[4,16,128]{2,1,0:T(8,128)} %class_hbm.1, f32[16]{0:T(128)} %shift_hbm.1, s32[1,128]{1,0:T(1,128)} %bitcast.3, s32[1,1]{1,0:T(1,128)} %bitcast.2.live_hbm, ...), custom_call_target="tpu_custom_call" | custom-call | tf_op jit(solution)/shard_map/pallas_call | solution.py:689
  27.8 0.7 %shard_map.87 = (f32[8,4,16,128]{3,2,1,0:T(8,128)}, f32[8,128]{1,0:T(8,128)}) custom-call(f32[4,16,8,128]{3,2,1,0:T(8,128)S(1)} %get-tuple-element.4.field_v, f32[8,128]{1,0:T(8,128)S(1)} %get-tuple-element.5.potential_v), custom_call_target="tpu_custom_call" | custom-call | tf_op jit(solution)/shard_map/pallas_call | solution.py:747

commit v4 on v3

--- a/solution.py
+++ b/solution.py
@@ -55,7 +55,7 @@
     init_v, source_v, forcing_v, class_v, weight_v, state_v,
     x_out, x_in, y_out, y_in, z_out, z_in, xy_in, xz_in, yz_in,
     wx_out, wx_in, wy_out, wy_in, wz_out, wz_in, rim_x, rim_y, rim_z,
-    rim_wx, rim_wy, rim_wz,
+    rim_wx, rim_wy, rim_wz, meter,
     geo_all, column_v, tile_v, density_out, density_all, at_cell,
     shift_ref, live_ref, cell_ref, geo_ref,
     known, local_sem, face_send, face_recv, gather_send, geo_recv, density_recv,
@@ -70,6 +70,17 @@
     here = tuple(lax.axis_index(axis) for axis in AXES)
     me = (here[0] * cols + here[1]) * depths + here[2]
 
+    def brick_copies(hbm, vmem, sem):
+        return [
+            pltpu.make_async_copy(hbm.at[e], vmem.at[:, :, e, :], sem) for e in range(channels)
+        ]
+
+    def brick_wait(vmem, sem):
+        pltpu.make_async_copy(vmem, vmem, sem).wait()
+
+    for copy in brick_copies(init_hbm, init_v, local_sem.at[0]):
+        copy.start()
+
     reach = max(1, rows // 4)
     barrier = pltpu.get_barrier_semaphore()
 
@@ -109,14 +120,6 @@
         told = jnp.where(here[0] + d < rows - 1, 1, 0) + jnp.where(here[0] > d, 1, 0)
         pl.when(told > 0)(lambda: pl.semaphore_wait(known.at[stage], told))
 
-    def brick_copies(hbm, vmem, sem):
-        return [
-            pltpu.make_async_copy(hbm.at[e], vmem.at[:, :, e, :], sem) for e in range(channels)
-        ]
-
-    def brick_wait(vmem, sem):
-        pltpu.make_async_copy(vmem, vmem, sem).wait()
-
     copies = [
         pltpu.make_async_copy(class_hbm, class_v, local_sem.at[1]),
         pltpu.make_async_copy(geo_hbm, geo_ref, local_sem.at[3]),
@@ -124,10 +127,6 @@
         pltpu.make_async_copy(cell_hbm, cell_ref, local_sem.at[5]),
         pltpu.make_async_copy(live_hbm, live_ref, local_sem.at[6]),
     ]
-    for copy in brick_copies(init_hbm, init_v, local_sem.at[0]):
-        copy.start()
-    for copy in copies:
-        copy.start()
 
     def nth(k):
         below, above = here[0], rows - 1 - here[0]
@@ -150,146 +149,136 @@
         lax.fori_loop(0, rows - 1, others, 0)
         at(here[0], True)
 
+    for copy in copies:
+        copy.start()
     for copy in brick_copies(source_hbm, source_v, local_sem.at[2]):
         copy.start()
 
-    cell_shape = (channels, size_z)
-    lane = lax.broadcasted_iota(jnp.int32, cell_shape, 1)
-    pair = lane >> 1
+    cell_shape, pair_shape = (channels, size_z), (2 * channels, size_z)
+    pairs = size_y // 2
+    lane = lax.broadcasted_iota(jnp.int32, pair_shape, 1)
     even = (lane & 1) == 0
-    edge = (lane == 0) | (lane == size_z - 1)
+    at_pair = lane >> 1
+    in_line = lax.rem(at_pair, pairs)
+    upper = lax.broadcasted_iota(jnp.int32, pair_shape, 0) < channels
+    low_plane = at_pair < pairs
+    high_plane = (at_pair >= (size_x - 1) * pairs) & (at_pair < size_x * pairs)
+    edge = jnp.where((lane == 0) | (lane == size_z - 1), 1.0, 0.0).astype(jnp.bfloat16)
     slab = (size_y * channels, size_z)
     slab_lane = lax.broadcasted_iota(jnp.int32, slab, 1)
-    first_line = lax.rem(pair, size_y) == 0
-    last_line = lax.rem(pair, size_y) == size_y - 1
-    low_plane, high_plane = pair < size_y, pair >= (size_x - 1) * size_y
 
     def turn(value, shift):
         return pltpu.roll(value, shift % size_z, 1)
 
-    def half_of_pair(i):
-        return slice(channels * (i % 2), channels * (i % 2) + channels)
-
-    def pack_deep(values):
-        packed = jnp.zeros(cell_shape, jnp.float32)
-        for x in range(size_x):
-            for y in range(size_y):
-                at = x * size_y + y
-                packed = jnp.where(pair == at, turn(values[x][y], 2 * at + 1), packed)
-        return packed
+    def swap(value):
+        return jnp.concatenate([value[channels:], value[:channels]], axis=0)
 
     def planes(ref):
         return [[ref[x, y] for y in range(size_y)] for x in range(size_x)]
 
+    def in_pairs(values):
+        return [
+            [
+                jnp.concatenate([line[y], line[y + 1]], axis=0).astype(jnp.bfloat16)
+                for y in range(0, size_y, 2)
+            ]
+            for line in values
+        ]
+
+    def pack_deep(paired):
+        packed = jnp.zeros(pair_shape, jnp.bfloat16)
+        for x in range(size_x):
+            for p in range(pairs):
+                packed = packed + turn(paired[x][p] * edge, 2 * (x * pairs + p) + 1)
+        return packed
+
     def pack(q, values):
+        paired = in_pairs(values)
         for side, x in ((0, 0), (1, size_x - 1)):
-            for y in range(0, size_y, 2):
-                both = jnp.concatenate([values[x][y], values[x][y + 1]], axis=0)
-                x_out[q, side, y // 2] = both.astype(x_out.dtype)
+            for p in range(pairs):
+                x_out[q, side, p] = paired[x][p]
         for side, y in ((0, 0), (1, size_y - 1)):
             for x in range(0, size_x, 2):
                 both = jnp.concatenate([values[x][y], values[x + 1][y]], axis=0)
                 y_out[q, side, x // 2] = both.astype(y_out.dtype)
-        z_out[q] = pack_deep(values)
-
-    numbers = {}
-
-    def number(*key):
-        return numbers.setdefault(key, len(numbers))
-
-    def sided(axis, side):
-        return 0 if sizes[axis] == 2 else side
-
-    def there(axis, up):
-        return here[axis] + (1 if up else -1)
+        z_out[q] = pack_deep(paired)
 
     def exists(axis, up):
         return here[axis] < sizes[axis] - 1 if up else here[axis] > 0
 
-    faces = [(axis, up) for axis in range(3) if sizes[axis] > 1 for up in (0, 1)]
-    corners = [
-        (a, ua, b, ub)
-        for a, b in ((0, 1), (0, 2), (1, 2))
-        if sizes[a] > 1 and sizes[b] > 1
-        for ua in (0, 1)
-        for ub in (0, 1)
-    ]
+    beside = []
+    for axis in range(3):
+        if sizes[axis] == 2:
+            beside.append((axis, 1 - here[axis], 1 - here[axis], None))
+        elif sizes[axis] > 2:
+            beside.append((axis, 0, here[axis] - 1, exists(axis, 0)))
+            beside.append((axis, 1, here[axis] + 1, exists(axis, 1)))
+    edges_beside = [(one, two) for one in beside for two in beside if one[0] < two[0]]
     outs, ins = (x_out, y_out, z_out), (x_in, y_in, z_in)
     edge_ins = {(0, 1): xy_in, (0, 2): xz_in, (1, 2): yz_in}
 
-    def exchange(q, edges=False):
-        kind = q % 3
-        made = []
-
-        def add(source, landing, key_out, key_in, target, present):
-            send = functools.partial(
-                pltpu.make_async_remote_copy,
+    def when(present, action):
+        if present is None:
+            action()
+        else:
+            pl.when(present)(action)
+
+    def start(source, landing, sem, target, present):
+        def go():
+            pltpu.make_async_remote_copy(
                 src_ref=source,
-                dst_ref=landing[0],
+                dst_ref=landing,
                 send_sem=face_send.at[0],
-                recv_sem=face_recv.at[number(kind, *key_out)],
+                recv_sem=face_recv.at[sem],
                 device_id=target,
                 device_id_type=MESH,
-            )
-            wait = functools.partial(
-                pltpu.make_async_copy, landing[1], landing[1], face_recv.at[number(kind, *key_in)]
-            )
-            made.append((send, wait, present))
-
-        for axis, up in () if edges else faces:
-            source = outs[axis].at[q] if axis == 2 else outs[axis].at[q, up]
-            landing = [ins[axis].at[q, side] for side in (1 - up, up)]
-            add(
-                source, landing, (axis, sided(axis, 1 - up)), (axis, sided(axis, up)),
-                {AXES[axis]: there(axis, up)}, exists(axis, up),
-            )
-        for a, ua, b, ub in corners if edges else ():
+            ).start()
+
+        when(present, go)
+
+    def start_faces(q):
+        for axis, side, place, present in beside:
+            source = outs[axis].at[q] if axis == 2 else outs[axis].at[q, side]
+            start(source, ins[axis].at[q, 1 - side], q % 3, {AXES[axis]: place}, present)
+
+    def start_edges(q):
+        for (a, side_a, place_a, one), (b, side_b, place_b, two) in edges_beside:
             if (a, b) == (0, 1):
-                source = y_out.at[q, ub, (size_x - 1) // 2 if ua else 0]
+                source = y_out.at[q, side_b, side_a * ((size_x - 1) // 2)]
             else:
                 source = z_out.at[q]
-            into = edge_ins[a, b]
-            landing = [into.at[q // 3, 1 - ua, 1 - ub], into.at[q // 3, ua, ub]]
-            add(
-                source, landing,
-                (a, b, sided(a, 1 - ua), sided(b, 1 - ub)), (a, b, sided(a, ua), sided(b, ub)),
-                {AXES[a]: there(a, ua), AXES[b]: there(b, ub)}, exists(a, ua) & exists(b, ub),
-            )
-        return made
-
-    def weight_messages():
-        made = []
-        for axis, up in faces:
-            send_ref, receive = ((wx_out, wx_in), (wy_out, wy_in), (wz_out, wz_in))[axis]
-            source = send_ref if axis == 2 else send_ref.at[up]
-            send = functools.partial(
-                pltpu.make_async_remote_copy,
-                src_ref=source,
-                dst_ref=receive.at[1 - up],
-                send_sem=face_send.at[0],
-                recv_sem=face_recv.at[number("weight", axis, sided(axis, 1 - up))],
-                device_id={AXES[axis]: there(axis, up)},
-                device_id_type=MESH,
-            )
-            landed = receive.at[up]
-            wait = functools.partial(
-                pltpu.make_async_copy, landed, landed,
-                face_recv.at[number("weight", axis, sided(axis, up))],
-            )
-            made.append((send, wait, exists(axis, up)))
-        return made
-
-    def start(made):
-        for send, _, present in made:
-            pl.when(present)(lambda send=send: send().start())
-
-    def land(made):
-        for _, wait, present in made:
-            pl.when(present)(lambda wait=wait: wait().wait())
-
-    def drain(made):
-        for send, _, present in made:
-            pl.when(present)(lambda send=send: send().wait_send())
+            landing = edge_ins[a, b].at[q // 3, 1 - side_a, 1 - side_b]
+            present = two if one is None else one if two is None else one & two
+            start(source, landing, 3, {AXES[a]: place_a, AXES[b]: place_b}, present)
+
+    def start_weights():
+        for axis, side, place, present in beside:
+            out, into = ((wx_out, wx_in), (wy_out, wy_in), (wz_out, wz_in))[axis]
+            source = out if axis == 2 else out.at[side]
+            start(source, into.at[1 - side], 4, {AXES[axis]: place}, present)
+
+    def await_bytes(sem, each):
+        split = [axis for axis in range(3) if sizes[axis] > 2]
+        for case in range(2 ** len(split)):
+            counts = [min(count, 2) - 1 for count in sizes]
+            condition = None
+            for i, axis in enumerate(split):
+                both = (case >> i) & 1
+                counts[axis] += both
+                holds = (here[axis] > 0) & (here[axis] < sizes[axis] - 1)
+                holds = holds if both else jnp.logical_not(holds)
+                condition = holds if condition is None else condition & holds
+            span = meter.at[pl.ds(0, each(counts))]
+            when(condition, lambda span=span: pltpu.make_async_copy(span, span, sem).wait())
+
+    def face_cells(n):
+        return n[0] * pairs + n[1] * (size_x // 2) + n[2]
+
+    def edge_cells(n):
+        return n[0] * n[1] + n[0] * n[2] + n[1] * n[2]
+
+    def weight_cells(n):
+        return n[0] * (size_y // channels) + n[1] + n[2]
 
     none = 3 * ROUNDS
     x_in[none] = jnp.zeros(x_in.shape[1:], x_in.dtype)
@@ -306,6 +295,12 @@
 
     pack(0, planes(init_v))
 
+    with jax.named_scope("w_barrier"):
+        pl.semaphore_wait(barrier, near)
+    if stages:
+        pass_on(0)
+    start_faces(0)
+
     copies[1].wait()
     eye = lax.broadcasted_iota(jnp.int32, (slots, slots), 0) == lax.broadcasted_iota(
         jnp.int32, (slots, slots), 1
@@ -313,13 +308,8 @@
     for i in range(3):
         column = jnp.sum(jnp.where(eye, geo_ref[i : i + 1, :], 0.0), axis=1, keepdims=True)
         column_v[i] = jnp.broadcast_to(column, (slots, slots))
-    geo_all[me] = geo_ref[...]
-
-    with jax.named_scope("w_barrier"):
-        pl.semaphore_wait(barrier, near)
-    if stages:
-        pass_on(0)
-    start(exchange(0))
+    pltpu.make_async_copy(geo_ref, geo_all.at[me], geo_recv.at[here[0]]).start()
+
 
     def start_gather(source, gathered, sem):
         def send(device):
@@ -351,10 +341,12 @@
             wx_out[0] = weight
         if x == size_x - 1:
             wx_out[1] = weight
+        if x == 0:
+            wy_out[...] = jnp.zeros(wy_out.shape, wy_out.dtype)
         wy_out[0, x : x + 1, :] = weight[0:1]
         wy_out[1, x : x + 1, :] = weight[size_y - 1 : size_y]
-    wz_out[...] = pack_deep(planes(weight_v))
-    start(weight_messages())
+    wz_out[...] = pack_deep(in_pairs(planes(weight_v)))
+    start_weights()
 
     copies[3].wait()
     copies[4].wait()
@@ -386,7 +378,8 @@
         return around + beside.reshape(value.shape)
 
     def ends(beyond, at):
-        return jnp.where(edge, turn(beyond, -2 * at), 0.0)
+        both = (turn(beyond, -2 * at) * edge).astype(jnp.float32)
+        return both[:channels], both[channels:]
 
     def inner(source, target, force):
         for x in range(size_x):
@@ -404,6 +397,9 @@
             jnp.where(here[axis] < sizes[axis] - 1, q, none),
         )
 
+    def half_of_pair(i):
+        return slice(channels * (i % 2), channels * (i % 2) + channels)
+
     def from_x(q, side, y):
         both = x_in[pick(0, q)[side], side, y // 2].astype(jnp.float32)
         return both[half_of_pair(y)]
@@ -412,48 +408,50 @@
         both = y_in[pick(1, q)[side], side, x // 2].astype(jnp.float32)
         return both[half_of_pair(x)]
 
+    def either(low, high):
+        return jnp.where(even, low.astype(jnp.float32), high.astype(jnp.float32))
+
     def from_z(q):
         below, above = pick(2, q)
-        return jnp.where(even, z_in[below, 0], z_in[above, 1])
+        return either(z_in[below, 0], z_in[above, 1])
 
     def beside_ends(natural):
-        return jnp.where(even, natural, turn(natural, -2))
+        return jnp.where(even, natural, turn(natural, -2)).astype(jnp.bfloat16)
 
     def corner(a, b, q, side_a, side_b):
-        there_a = here[a] > 0 if side_a == 0 else here[a] < sizes[a] - 1
-        there_b = here[b] > 0 if side_b == 0 else here[b] < sizes[b] - 1
-        return edge_ins[a, b][jnp.where(there_a & there_b, q // 3, ROUNDS), side_a, side_b]
+        there = exists(a, side_a) & exists(b, side_b)
+        return edge_ins[a, b][jnp.where(there, q // 3, ROUNDS), side_a, side_b]
 
     def corner_xy(q, side_x, side_y):
         both = corner(0, 1, q, side_x, side_y).astype(jnp.float32)
         return both[half_of_pair(size_x - 1 if side_x == 0 else 0)]
 
     def corner_z(axis, q, side):
-        return jnp.where(even, corner(axis, 2, q, side, 0), corner(axis, 2, q, side, 1))
+        return either(corner(axis, 2, q, side, 0), corner(axis, 2, q, side, 1))
 
     def outer(target, q):
         beyond = beside_ends(from_z(q))
         for x in range(size_x):
-            for y in range(size_y):
-                around = ends(beyond, x * size_y + y)
-                if x == 0:
-                    around = around + from_x(q, 0, y)
-                if x == size_x - 1:
-                    around = around + from_x(q, 1, y)
-                if y == 0:
-                    around = around + from_y(q, 0, x)
-                if y == size_y - 1:
-                    around = around + from_y(q, 1, x)
-                target[x, y] = target[x, y] + weight_v[x, y] * around
+            for p in range(pairs):
+                for y, around in zip((2 * p, 2 * p + 1), ends(beyond, x * pairs + p)):
+                    if x == 0:
+                        around = around + from_x(q, 0, y)
+                    if x == size_x - 1:
+                        around = around + from_x(q, 1, y)
+                    if y == 0:
+                        around = around + from_y(q, 0, x)
+                    if y == size_y - 1:
+                        around = around + from_y(q, 1, x)
+                    target[x, y] = target[x, y] + weight_v[x, y] * around
 
     def spread_weights():
         for side in (0, 1):
             weight = wx_in[jnp.where(exists(0, side), side, 2)]
             rim_wx[side] = jnp.broadcast_to(weight[:, None, :], (size_y,) + cell_shape)
-            weight = wy_in[jnp.where(exists(1, side), side, 2)]
+            weight = wy_in[jnp.where(exists(1, side), side, 2)][:size_x]
             rim_wy[side] = jnp.broadcast_to(weight[:, None, :], (size_x,) + cell_shape)
-        rim_wz[...] = jnp.where(
-            even, wz_in[jnp.where(exists(2, 0), 0, 2)], wz_in[jnp.where(exists(2, 1), 1, 2)]
+        rim_wz[...] = either(
+            wz_in[jnp.where(exists(2, 0), 0, 2)], wz_in[jnp.where(exists(2, 1), 1, 2)]
         )
 
     def own_rim(source, q):
@@ -461,57 +459,64 @@
             rim_x[side] = rim_wx[side] * source[(size_x - 1) * side]
             for x in range(size_x):
                 rim_y[side, x] = rim_wy[side, x] * source[x, (size_y - 1) * side]
-        own = z_out[q]
+        own = z_out[q].astype(jnp.float32)
         rim_z[...] = rim_wz[...] * jnp.where(even, turn(own, -1), turn(own, 1))
 
-    def edge_rim(q):
-        for side in (0, 1):
-            across = beside_ends(corner_z(0, q, side))
+    def rim(target, q):
+        along, across = (size_x - 1) * size_y, 2 * (pairs - 1)
+        around = jnp.where(low_plane, turn(corner_z(0, q, 0), -along), 0.0)
+        around = around + jnp.where(high_plane, turn(corner_z(0, q, 1), along), 0.0)
+        first = upper & (in_line == 0)
+        final = jnp.logical_not(upper) & (in_line == pairs - 1)
+        around = around + jnp.where(first, swap(turn(corner_z(1, q, 0), -across)), 0.0)
+        around = around + jnp.where(final, swap(turn(corner_z(1, q, 1), across)), 0.0)
+        beyond = beside_ends(rim_z[...] + rim_wz[...] * around + from_z(q + 1))
+        beyond_x = [beside_ends(corner_z(0, q, side)) for side in (0, 1)]
+        beyond_y = [beside_ends(corner_z(1, q, side)) for side in (0, 1)]
+
+        def swept_x(side, p):
+            found = []
             theirs = (size_x - 1) * (1 - side)
-            for y in range(size_y):
-                around = ends(across, theirs * size_y + y)
+            for y, around in zip((2 * p, 2 * p + 1), ends(beyond_x[side], theirs * pairs + p)):
                 if y == 0:
                     around = around + corner_xy(q, side, 0)
                 if y == size_y - 1:
                     around = around + corner_xy(q, side, 1)
-                rim_x[side, y] = rim_x[side, y] + rim_wx[side, y] * around
-        for side in (0, 1):
-            across = beside_ends(corner_z(1, q, side))
+                found.append(rim_x[side, y] + from_x(q + 1, side, y) + rim_wx[side, y] * around)
+            return found
+
+        def swept_y(side, x):
             theirs = (size_y - 1) * (1 - side)
-            for x in range(size_x):
-                around = ends(across, x * size_y + theirs)
-                if x == 0:
-                    around = around + corner_xy(q, 0, side)
-                if x == size_x - 1:
-                    around = around + corner_xy(q, 1, side)
-                rim_y[side, x] = rim_y[side, x] + rim_wy[side, x] * around
-        step, wrap = 2 * size_y, 2 * (size_y - 1)
-        around = turn(jnp.where(high_plane, corner_z(0, q, 0), 0.0), step)
-        around = around + turn(jnp.where(low_plane, corner_z(0, q, 1), 0.0), -step)
-        around = around + jnp.where(first_line, turn(corner_z(1, q, 0), -wrap), 0.0)
-        around = around + jnp.where(last_line, turn(corner_z(1, q, 1), wrap), 0.0)
-        rim_z[...] = rim_z[...] + rim_wz[...] * around
-
-    def add_rim(target, q):
-        beyond = beside_ends(rim_z[...] + from_z(q))
+            around = ends(beyond_y[side], x * pairs + theirs // 2)[theirs % 2]
+            if x == 0:
+                around = around + corner_xy(q, 0, side)
+            if x == size_x - 1:
+                around = around + corner_xy(q, 1, side)
+            return rim_y[side, x] + from_y(q + 1, side, x) + rim_wy[side, x] * around
+
         for x in range(size_x):
-            for y in range(size_y):
-                around = ends(beyond, x * size_y + y)
-                if x == 0:
-                    around = around + (rim_x[0, y] + from_x(q, 0, y))
-                if x == size_x - 1:
-                    around = around + (rim_x[1, y] + from_x(q, 1, y))
-                if y == 0:
-                    around = around + (rim_y[0, x] + from_y(q, 0, x))
-                if y == size_y - 1:
-                    around = around + (rim_y[1, x] + from_y(q, 1, x))
-                target[x, y] = target[x, y] + weight_v[x, y] * around
+            for p in range(pairs):
+                below = swept_x(0, p) if x == 0 else None
+                above = swept_x(1, p) if x == size_x - 1 else None
+                for i, around in enumerate(ends(beyond, x * pairs + p)):
+                    y = 2 * p + i
+                    if below:
+                        around = around + below[i]
+                    if above:
+                        around = around + above[i]
+                    if y == 0:
+                        around = around + swept_y(0, x)
+                    if y == size_y - 1:
+                        around = around + swept_y(1, x)
+                    target[x, y] = target[x, y] + weight_v[x, y] * around
 
     pieces = 4
     chunk = slots // pieces
 
-    def make_tiles(first, stop):
-        def body(q, carry):
+    def make_tiles():
+        def body(k, carry):
+            q = nth(k)
+            await_gather(geo_all, group, geo_recv.at[q])
             for j in range(group):
                 source = geo_all[q * group + j]
                 for piece in range(pieces):
@@ -526,7 +531,7 @@
                     tile_v[q, span, j * slots : (j + 1) * slots] = value.astype(tile_v.dtype)
             return carry
 
-        lax.fori_loop(first, stop, body, 0)
+        lax.fori_loop(0, rows, body, 0)
 
     def apply_tiles(r):
         total = jnp.zeros((channels, slots), jnp.float32)
@@ -542,12 +547,18 @@
             )
         return total
 
+    def land(sem, each):
+        await_bytes(face_recv.at[sem], each)
+
+    def drain(each):
+        await_bytes(face_send.at[0], each)
+
     def drain_now():
         for q in range(3 * ROUNDS - 2):
-            drain(exchange(q))
+            drain(face_cells)
             if q % 3 == 1:
-                drain(exchange(q, edges=True))
-        drain(weight_messages())
+                drain(edge_cells)
+        drain(weight_cells)
         await_gather(geo_all, devices - 1, gather_send.at[0])
         for r in range(ROUNDS - 1):
             await_gather(density_all.at[r], devices - 1, gather_send.at[0])
@@ -563,15 +574,14 @@
             inner(before, once, forcing_v.at[0])
         if r > 0:
             with jax.named_scope("tilesB"):
-                await_gather(geo_all, devices - 1, geo_recv.at[0])
-                make_tiles(0, rows)
+                make_tiles()
         if r == 0:
             with jax.named_scope("w_known0"):
                 for stage in range(len(stages) - 1):
                     hear(stage)
                     pass_on(stage + 1)
         with jax.named_scope(f"w_single{r}"):
-            land(exchange(single))
+            land(0, face_cells)
         with jax.named_scope(f"outer{r}"):
             outer(once, single)
         if r > 0:
@@ -595,38 +605,36 @@
                     once[x] = once[x] + change
         with jax.named_scope(f"pack{r}"):
             pack(double, planes(once))
-        start(exchange(double, edges=True))
-        start(exchange(double))
+        start_edges(double)
+        start_faces(double)
         with jax.named_scope(f"innerd{r}"):
             inner(once, mid, force)
         with jax.named_scope(f"packd{r}"):
             pack(double + 1, planes(mid))
-        start(exchange(double + 1))
+        start_faces(double + 1)
         if r == 0:
             with jax.named_scope("w_weights"):
-                land(weight_messages())
+                land(4, weight_cells)
                 spread_weights()
             with jax.named_scope("w_known"):
                 if stages:
                     hear(len(stages) - 1)
             with jax.named_scope("st_geo"):
-                start_gather(geo_ref, geo_all, geo_recv.at[0])
+                start_gather(geo_ref, geo_all, geo_recv.at[here[0]])
         else:
             drain_now()
         own_rim(once, double)
         with jax.named_scope(f"w_double{r}"):
-            land(exchange(double))
+            land(1, face_cells)
         with jax.named_scope(f"outerd{r}"):
             outer(mid, double)
             inner(mid, after, force)
         with jax.named_scope(f"w_edges{r}"):
-            land(exchange(double, edges=True))
-        with jax.named_scope(f"before_rim{r}"):
-            edge_rim(double)
+            land(3, edge_cells)
         with jax.named_scope(f"w_rim{r}"):
-            land(exchange(double + 1))
+            land(2, face_cells)
         with jax.named_scope(f"rim{r}"):
-            add_rim(after, double + 1)
+            rim(after, double)
         with jax.named_scope(f"density{r}"):
             flat = after[...].reshape(size_x * size_y * channels, size_z).astype(jnp.bfloat16)
             picked = jnp.dot(flat, pick_z, preferred_element_type=jnp.float32)
@@ -640,10 +648,10 @@
         if r < ROUNDS - 1:
             with jax.named_scope(f"pack_s{r}"):
                 pack(single + 3, planes(after))
-            start(exchange(single + 3))
-    drain(exchange(3 * ROUNDS - 2))
-    drain(exchange(3 * ROUNDS - 2, edges=True))
-    drain(exchange(3 * ROUNDS - 1))
+            start_faces(single + 3)
+    drain(face_cells)
+    drain(edge_cells)
+    drain(face_cells)
     with jax.named_scope(f"apply{ROUNDS-1}"):
         potential_ref[...] = jnp.where(live, apply_tiles(ROUNDS - 1), 0.0)
 
@@ -684,8 +692,6 @@
     ]
     operands.insert(5, live_count.reshape(1, 1))
     two, turns = 2 * channels, 3 * ROUNDS
-    sides = [min(count, 3) - 1 for count in sizes]
-    crossed = sides[0] * sides[1] + sides[0] * sides[2] + sides[1] * sides[2]
     field, potential = pl.pallas_call(
         functools.partial(kernel, sizes),
         out_shape=(
@@ -705,23 +711,24 @@
             pltpu.VMEM((turns + 1, 2, size_y // 2, two, size_z), jnp.bfloat16),
             pltpu.VMEM((turns, 2, size_x // 2, two, size_z), jnp.bfloat16),
             pltpu.VMEM((turns + 1, 2, size_x // 2, two, size_z), jnp.bfloat16),
-            pltpu.VMEM((turns, channels, size_z), jnp.float32),
-            pltpu.VMEM((turns + 1, 2, channels, size_z), jnp.float32),
+            pltpu.VMEM((turns, two, size_z), jnp.bfloat16),
+            pltpu.VMEM((turns + 1, 2, two, size_z), jnp.bfloat16),
             pltpu.VMEM((ROUNDS + 1, 2, 2, two, size_z), jnp.bfloat16),
-            pltpu.VMEM((ROUNDS + 1, 2, 2, channels, size_z), jnp.float32),
-            pltpu.VMEM((ROUNDS + 1, 2, 2, channels, size_z), jnp.float32),
+            pltpu.VMEM((ROUNDS + 1, 2, 2, two, size_z), jnp.bfloat16),
+            pltpu.VMEM((ROUNDS + 1, 2, 2, two, size_z), jnp.bfloat16),
             pltpu.VMEM((2, size_y, size_z), jnp.float32),
             pltpu.VMEM((3, size_y, size_z), jnp.float32),
-            pltpu.VMEM((2, size_x, size_z), jnp.float32),
-            pltpu.VMEM((3, size_x, size_z), jnp.float32),
-            pltpu.VMEM((channels, size_z), jnp.float32),
+            pltpu.VMEM((2, channels, size_z), jnp.float32),
             pltpu.VMEM((3, channels, size_z), jnp.float32),
+            pltpu.VMEM((two, size_z), jnp.bfloat16),
+            pltpu.VMEM((3, two, size_z), jnp.bfloat16),
             pltpu.VMEM((2, size_y, channels, size_z), jnp.float32),
             pltpu.VMEM((2, size_x, channels, size_z), jnp.float32),
-            pltpu.VMEM((channels, size_z), jnp.float32),
+            pltpu.VMEM((two, size_z), jnp.float32),
             pltpu.VMEM((2, size_y, channels, size_z), jnp.float32),
             pltpu.VMEM((2, size_x, channels, size_z), jnp.float32),
-            pltpu.VMEM((channels, size_z), jnp.float32),
+            pltpu.VMEM((two, size_z), jnp.float32),
+            pltpu.VMEM((size_y + size_x + 2, channels, size_z), jnp.float32),
             pltpu.VMEM((devices, 4, slots), jnp.float32),
             pltpu.VMEM((3, slots, slots), jnp.float32),
             pltpu.VMEM((rows, slots, group * slots), jnp.bfloat16),
@@ -735,9 +742,9 @@
             pltpu.SemaphoreType.REGULAR((max(1, len(known_stages(rows))),)),
             pltpu.SemaphoreType.DMA((7,)),
             pltpu.SemaphoreType.DMA((1,)),
-            pltpu.SemaphoreType.DMA((4 * sum(sides) + crossed,)),
+            pltpu.SemaphoreType.DMA((5,)),
             pltpu.SemaphoreType.DMA((1,)),
-            pltpu.SemaphoreType.DMA((1,)),
+            pltpu.SemaphoreType.DMA((rows,)),
             pltpu.SemaphoreType.DMA((ROUNDS, rows)),
         ],
         compiler_params=pltpu.CompilerParams(

time: 28.7 us -> 28.5 us (level)
  Pallas kernels: 27.3 us -> 27 us
where the time goes in v4:
time: 28.5 us; the launch traced here: 28.3 us
  Pallas kernels  27 us (95%)
  between operations  1.29 us (5%)
    pallas_call x1, Pallas kernels, local(): pl.pallas_call(functools.partial(kernel, sizes), out_shape=(jax.ShapeDtyp...  26.3 us
    pallas_call x1, Pallas kernels, local(): pl.pallas_call(place, out_shape=(jax.ShapeDtypeStruct(initial_field.shape...  0.71 us

profile of v4, /device:TPU:0, one launch (start us, length us, event | category | flops | bytes accessed | tf_op | source)
XLA Modules:
  0.0 28.3 jit_solution(13076870803561335274)
XLA Ops:
  1.3 26.3 %shard_map.86 = (f32[4,16,8,128]{3,2,1,0:T(8,128)S(1)}, f32[8,128]{1,0:T(8,128)S(1)}) custom-call(f32[8,4,16,128]{3,2,1,0:T(8,128)} %init_hbm.1, f32[8,4,16,128]{3,2,1,0:T(8,128)} %source_hbm.1, s32[4,16,128]{2,1,0:T(8,128)} %class_hbm.1, f32[16]{0:T(128)} %shift_hbm.1, s32[1,128]{1,0:T(1,128)} %bitcast.3, s32[1,1]{1,0:T(1,128)} %bitcast.2.live_hbm, ...), custom_call_target="tpu_custom_call" | custom-call | tf_op jit(solution)/shard_map/pallas_call | solution.py:695
  27.6 0.7 %shard_map.87 = (f32[8,4,16,128]{3,2,1,0:T(8,128)}, f32[8,128]{1,0:T(8,128)}) custom-call(f32[4,16,8,128]{3,2,1,0:T(8,128)S(1)} %get-tuple-element.4.field_v, f32[8,128]{1,0:T(8,128)S(1)} %get-tuple-element.5.potential_v), custom_call_target="tpu_custom_call" | custom-call | tf_op jit(solution)/shard_map/pallas_call | solution.py:754

commit v5 on v4

--- a/solution.py
+++ b/solution.py
@@ -41,7 +41,7 @@
 
 
 def known_stages(rows):
-    stages, reach = [], max(1, rows // 4)
+    stages, reach = [], max(1, rows // 8)
     while reach < rows - 1:
         stages.append(reach)
         reach *= 2
@@ -81,7 +81,7 @@
     for copy in brick_copies(init_hbm, init_v, local_sem.at[0]):
         copy.start()
 
-    reach = max(1, rows // 4)
+    reach = max(1, rows // 8)
     barrier = pltpu.get_barrier_semaphore()
 
     def greet(row, first):
@@ -128,11 +128,14 @@
         pltpu.make_async_copy(live_hbm, live_ref, local_sem.at[6]),
     ]
 
+    def nearest(k, own, count):
+        below, above = own, count - 1 - own
+        near = own + jnp.where(lax.rem(k, 2) == 1, (k + 1) // 2, -(k // 2))
+        far = jnp.where(below < above, k, count - 1 - k)
+        return jnp.where((k <= 2 * below) & (k <= 2 * above), near, far)
+
     def nth(k):
-        below, above = here[0], rows - 1 - here[0]
-        near = here[0] + jnp.where(lax.rem(k, 2) == 1, (k + 1) // 2, -(k // 2))
-        far = jnp.where(below < above, k, rows - 1 - k)
-        return jnp.where((k <= 2 * below) & (k <= 2 * above), near, far)
+        return nearest(k, here[0], rows)
 
     def each_other(action):
         def at(row, first):
@@ -310,6 +313,44 @@
         column_v[i] = jnp.broadcast_to(column, (slots, slots))
     pltpu.make_async_copy(geo_ref, geo_all.at[me], geo_recv.at[here[0]]).start()
 
+
+    fold = 2 - rows % 2
+    layers, layer, part = rows // fold, here[0] // fold, lax.rem(here[0], fold)
+
+    def start_geometry(known_before, known_now):
+        def to_row(row, first):
+            for b in reversed(range(cols)):
+                for c in reversed(range(depths)):
+                    if first and b == 0 and c == 0:
+                        continue
+                    pltpu.make_async_remote_copy(
+                        src_ref=geo_ref,
+                        dst_ref=geo_all.at[me],
+                        send_sem=gather_send.at[0],
+                        recv_sem=geo_recv.at[here[0]],
+                        device_id=(
+                            row, lax.rem(here[1] + b, cols), lax.rem(here[2] + c, depths)
+                        ),
+                        device_id_type=MESH,
+                    ).start()
+
+        if known_before < 0:
+            to_row(here[0], True)
+        for away in range(max(0, known_before) // fold + 1, min(known_now // fold, layers - 1) + 1):
+            away = away * fold
+            pl.when(here[0] >= away)(lambda: to_row(here[0] - away, False))
+            pl.when(here[0] + away < rows)(lambda: to_row(here[0] + away, False))
+
+    def hand_over(q):
+        blocks = geo_all.at[pl.ds(q * group, group)]
+        pltpu.make_async_remote_copy(
+            src_ref=blocks,
+            dst_ref=blocks,
+            send_sem=gather_send.at[0],
+            recv_sem=geo_recv.at[q],
+            device_id={"row": layer * fold + (fold - 1 - part)},
+            device_id_type=MESH,
+        ).start()
 
     def start_gather(source, gathered, sem):
         def send(device):
@@ -514,9 +555,12 @@
     chunk = slots // pieces
 
     def make_tiles():
-        def body(k, carry):
-            q = nth(k)
+        def body(i, carry):
+            a, k = i // layers, lax.rem(i, layers)
+            q = nearest(k, layer, layers) * fold + lax.rem(part + a, fold)
             await_gather(geo_all, group, geo_recv.at[q])
+            if fold > 1:
+                pl.when(a == 0)(lambda: hand_over(q))
             for j in range(group):
                 source = geo_all[q * group + j]
                 for piece in range(pieces):
@@ -563,6 +607,7 @@
         for r in range(ROUNDS - 1):
             await_gather(density_all.at[r], devices - 1, gather_send.at[0])
 
+    knowledge = ([rows, rows] + stages)[-2:] if len(stages) != 1 else stages * 2
     for r in range(ROUNDS):
         single, double = 3 * r, 3 * r + 1
         before = init_v if r == 0 else state_v.at[2]
@@ -577,11 +622,16 @@
                 make_tiles()
         if r == 0:
             with jax.named_scope("w_known0"):
-                for stage in range(len(stages) - 1):
+                for stage in range(len(stages) - 2):
                     hear(stage)
                     pass_on(stage + 1)
+                start_geometry(-1, knowledge[0])
         with jax.named_scope(f"w_single{r}"):
             land(0, face_cells)
+        if r == 0 and len(stages) > 1:
+            hear(len(stages) - 2)
+            pass_on(len(stages) - 1)
+            start_geometry(knowledge[0], knowledge[1])
         with jax.named_scope(f"outer{r}"):
             outer(once, single)
         if r > 0:
@@ -591,13 +641,14 @@
                 half_of = coupling * potential
                 big = half_of.astype(jnp.bfloat16).astype(jnp.float32)
                 small = half_of - big
-                load = jnp.zeros((size_x * size_y * channels, size_z), jnp.float32)
-                for part in (big, small):
-                    placed = (at_cell[...] * part[None]).astype(jnp.bfloat16)
-                    load = load + lax.dot_general(
-                        placed.reshape(size_x * size_y * channels, slots), pick_z,
-                        (((1,), (1,)), ((), ())), preferred_element_type=jnp.float32,
-                    )
+                placed = jnp.concatenate(
+                    [(at_cell[...] * part[None]).astype(jnp.bfloat16) for part in (big, small)],
+                    axis=2,
+                ).reshape(size_x * size_y * channels, 2 * slots)
+                load = lax.dot_general(
+                    placed, jnp.concatenate([pick_z, pick_z], axis=1),
+                    (((1,), (1,)), ((), ())), preferred_element_type=jnp.float32,
+                )
                 load = load.reshape(size_x, size_y, channels, size_z)
                 for x in range(size_x):
                     change = weight_v[x] * load[x]
@@ -620,7 +671,7 @@
                 if stages:
                     hear(len(stages) - 1)
             with jax.named_scope("st_geo"):
-                start_gather(geo_ref, geo_all, geo_recv.at[here[0]])
+                start_geometry(knowledge[1], rows)
         else:
             drain_now()
         own_rim(once, double)

time: 28.5 us -> 27.6 us (0.968)
  Pallas kernels: 27 us -> 26.1 us
    pallas_call x1, Pallas kernels: 26.3 us -> 25.4 us  [local(): pl.pallas_call(functools.partial(kernel, sizes), out_shape=(jax.ShapeDtyp...]
where the time goes in v5:
time: 27.6 us; the launch traced here: 27.4 us
  Pallas kernels  26.1 us (95%)
  between operations  1.29 us (5%)
    pallas_call x1, Pallas kernels, local(): pl.pallas_call(functools.partial(kernel, sizes), out_shape=(jax.ShapeDtyp...  25.4 us
    pallas_call x1, Pallas kernels, local(): pl.pallas_call(place, out_shape=(jax.ShapeDtypeStruct(initial_field.shape...  0.71 us

profile of v5, /device:TPU:0, one launch (start us, length us, event | category | flops | bytes accessed | tf_op | source)
XLA Modules:
  0.0 27.4 jit_solution(12667625265147763892)
XLA Ops:
  1.3 25.4 %shard_map.86 = (f32[4,16,8,128]{3,2,1,0:T(8,128)S(1)}, f32[8,128]{1,0:T(8,128)S(1)}) custom-call(f32[8,4,16,128]{3,2,1,0:T(8,128)} %init_hbm.1, f32[8,4,16,128]{3,2,1,0:T(8,128)} %source_hbm.1, s32[4,16,128]{2,1,0:T(8,128)} %class_hbm.1, f32[16]{0:T(128)} %shift_hbm.1, s32[1,128]{1,0:T(1,128)} %bitcast.3, s32[1,1]{1,0:T(1,128)} %bitcast.2.live_hbm, ...), custom_call_target="tpu_custom_call" | custom-call | tf_op jit(solution)/shard_map/pallas_call | solution.py:746
  26.7 0.7 %shard_map.87 = (f32[8,4,16,128]{3,2,1,0:T(8,128)}, f32[8,128]{1,0:T(8,128)}) custom-call(f32[4,16,8,128]{3,2,1,0:T(8,128)S(1)} %get-tuple-element.4.field_v, f32[8,128]{1,0:T(8,128)S(1)} %get-tuple-element.5.potential_v), custom_call_target="tpu_custom_call" | custom-call | tf_op jit(solution)/shard_map/pallas_call | solution.py:805

commit v6 on v5

--- a/solution.py
+++ b/solution.py
@@ -40,11 +40,41 @@
     return value
 
 
-def known_stages(rows):
-    stages, reach = [], max(1, rows // 8)
-    while reach < rows - 1:
-        stages.append(reach)
-        reach *= 2
+def relays(sizes):
+    rows, cols, depths = sizes
+    if cols != 2 or depths != 2 or rows < 2 or rows % 2:
+        return []
+    stages, far = [[(-1, 0, 0), (1, 0, 0), (0, 1, 0), (0, 0, 1)]], 2
+    while far < rows:
+        stages.append([(-far, 0, 0), (far, 0, 0)] + ([(0, 1, 1)] if far == 2 else []))
+        far *= 2
+    stages.append([(0, 1, 1)])
+
+    def at(device, offset):
+        r, c, d = (x + o for x, o in zip(device, offset))
+        return (r, c % 2, d % 2) if 0 <= r < rows else None
+
+    everyone = [(r, c, d) for r in range(rows) for c in range(2) for d in range(2)]
+    known = {x: {x} | {at(x, o) for o in stages[0]} for x in everyone}
+    for i, stage in enumerate(stages):
+        told = {x: set(known[x]) for x in everyone}
+        for x in everyone:
+            for offset in stage:
+                target = at(x, offset)
+                if target is not None:
+                    if target not in known[x]:
+                        return []
+                    told[target] |= known[x]
+        known = told
+        for x in everyone:
+            ahead = {at(x, (r, c, d)) for r in (-1, 0, 1) for c in (0, 1) for d in (0, 1) if abs(r) + c + d < 3}
+            ahead |= {at(x, (r, 0, 0)) for r in (-2, 2)}
+            if i == len(stages) - 2:
+                ahead = {y for y in everyone if (y[0] - x[0]) % 2 == 0}
+            if i == len(stages) - 1:
+                ahead = set(everyone)
+            if not ahead - {None} <= known[x] | {None}:
+                return []
     return stages
 
 
@@ -81,44 +111,52 @@
     for copy in brick_copies(init_hbm, init_v, local_sem.at[0]):
         copy.start()
 
-    reach = max(1, rows // 8)
+    stages = relays(sizes)
     barrier = pltpu.get_barrier_semaphore()
 
-    def greet(row, first):
-        for b in range(cols):
-            for c in range(depths):
-                if first and b == 0 and c == 0:
-                    continue
-                pl.semaphore_signal(
-                    barrier, inc=1, device_id_type=MESH,
-                    device_id=(row, lax.rem(here[1] + b, cols), lax.rem(here[2] + c, depths)),
-                )
-
-    greet(here[0], True)
-    for away in range(1, reach + 1):
-        pl.when(here[0] >= away)(lambda: greet(here[0] - away, False))
-        pl.when(here[0] + away < rows)(lambda: greet(here[0] + away, False))
-    near_low = jnp.where(here[0] > reach, here[0] - reach, 0)
-    near_high = jnp.where(here[0] + reach < rows, here[0] + reach, rows - 1)
-    near = (near_high - near_low + 1) * group - 1
-
-    stages = known_stages(rows)
+    def offset_place(offset):
+        return (
+            here[0] + offset[0],
+            1 - here[1] if offset[1] else here[1],
+            1 - here[2] if offset[2] else here[2],
+        )
+
+    def reaches(offset):
+        if offset[0] == 0:
+            return None
+        return here[0] >= -offset[0] if offset[0] < 0 else here[0] + offset[0] < rows
+
+    def tell(sem, offset):
+        def go():
+            pl.semaphore_signal(
+                sem, inc=1, device_id=offset_place(offset), device_id_type=MESH
+            )
+
+        present = reaches(offset)
+        if present is None:
+            go()
+        else:
+            pl.when(present)(go)
+
+    def tellers(stage):
+        return sum(
+            1 if reaches(offset) is None else jnp.where(reaches(offset), 1, 0)
+            for offset in stages[stage]
+        )
 
     def pass_on(stage):
-        d = stages[stage]
-
-        def tell(row):
-            pl.semaphore_signal(
-                known.at[stage], inc=1, device_id={"row": row}, device_id_type=MESH
-            )
-
-        pl.when((here[0] >= d) & (here[0] < rows - 1))(lambda: tell(here[0] - d))
-        pl.when((here[0] + d < rows) & (here[0] > 0))(lambda: tell(here[0] + d))
+        for offset in stages[stage]:
+            tell(known.at[stage], offset)
 
     def hear(stage):
-        d = stages[stage]
-        told = jnp.where(here[0] + d < rows - 1, 1, 0) + jnp.where(here[0] > d, 1, 0)
-        pl.when(told > 0)(lambda: pl.semaphore_wait(known.at[stage], told))
+        pl.semaphore_wait(known.at[stage], tellers(stage))
+
+    if stages:
+        for offset in stages[0]:
+            tell(barrier, offset)
+        near = tellers(0)
+    else:
+        near = devices - 1
 
     copies = [
         pltpu.make_async_copy(class_hbm, class_v, local_sem.at[1]),
@@ -152,6 +190,12 @@
         lax.fori_loop(0, rows - 1, others, 0)
         at(here[0], True)
 
+    if not stages:
+        each_other(
+            lambda device: pl.semaphore_signal(
+                barrier, inc=1, device_id=device, device_id_type=MESH
+            )
+        )
     for copy in copies:
         copy.start()
     for copy in brick_copies(source_hbm, source_v, local_sem.at[2]):
@@ -317,29 +361,36 @@
     fold = 2 - rows % 2
     layers, layer, part = rows // fold, here[0] // fold, lax.rem(here[0], fold)
 
-    def start_geometry(known_before, known_now):
-        def to_row(row, first):
-            for b in reversed(range(cols)):
-                for c in reversed(range(depths)):
-                    if first and b == 0 and c == 0:
-                        continue
-                    pltpu.make_async_remote_copy(
-                        src_ref=geo_ref,
-                        dst_ref=geo_all.at[me],
-                        send_sem=gather_send.at[0],
-                        recv_sem=geo_recv.at[here[0]],
-                        device_id=(
-                            row, lax.rem(here[1] + b, cols), lax.rem(here[2] + c, depths)
-                        ),
-                        device_id_type=MESH,
-                    ).start()
-
-        if known_before < 0:
-            to_row(here[0], True)
-        for away in range(max(0, known_before) // fold + 1, min(known_now // fold, layers - 1) + 1):
-            away = away * fold
-            pl.when(here[0] >= away)(lambda: to_row(here[0] - away, False))
-            pl.when(here[0] + away < rows)(lambda: to_row(here[0] + away, False))
+    def send_geometry(row, b, c):
+        pltpu.make_async_remote_copy(
+            src_ref=geo_ref,
+            dst_ref=geo_all.at[me],
+            send_sem=gather_send.at[0],
+            recv_sem=geo_recv.at[here[0]],
+            device_id=(row, lax.rem(here[1] + b, cols), lax.rem(here[2] + c, depths)),
+            device_id_type=MESH,
+        ).start()
+
+    others_beside = [(b, c) for b in range(cols) for c in range(depths)]
+
+    def start_geometry(near_part, far_part):
+        if near_part:
+            for b, c in others_beside[1:]:
+                send_geometry(here[0], b, c)
+        for away in reversed(range(fold, rows, fold)):
+            targets = []
+            if near_part and away == fold or far_part and away > fold:
+                targets += others_beside[:1]
+            if far_part:
+                targets += others_beside[1:]
+
+            def to_row(row, targets=targets):
+                for b, c in targets:
+                    send_geometry(row, b, c)
+
+            if targets:
+                pl.when(here[0] >= away)(lambda: to_row(here[0] - away))
+                pl.when(here[0] + away < rows)(lambda: to_row(here[0] + away))
 
     def hand_over(q):
         blocks = geo_all.at[pl.ds(q * group, group)]
@@ -607,7 +658,6 @@
         for r in range(ROUNDS - 1):
             await_gather(density_all.at[r], devices - 1, gather_send.at[0])
 
-    knowledge = ([rows, rows] + stages)[-2:] if len(stages) != 1 else stages * 2
     for r in range(ROUNDS):
         single, double = 3 * r, 3 * r + 1
         before = init_v if r == 0 else state_v.at[2]
@@ -622,16 +672,16 @@
                 make_tiles()
         if r == 0:
             with jax.named_scope("w_known0"):
-                for stage in range(len(stages) - 2):
-                    hear(stage)
-                    pass_on(stage + 1)
-                start_geometry(-1, knowledge[0])
+                if stages:
+                    hear(0)
+                    pass_on(1)
+                start_geometry(True, not stages)
         with jax.named_scope(f"w_single{r}"):
             land(0, face_cells)
-        if r == 0 and len(stages) > 1:
-            hear(len(stages) - 2)
-            pass_on(len(stages) - 1)
-            start_geometry(knowledge[0], knowledge[1])
+        if r == 0 and stages:
+            for stage in range(1, len(stages) - 2):
+                hear(stage)
+                pass_on(stage + 1)
         with jax.named_scope(f"outer{r}"):
             outer(once, single)
         if r > 0:
@@ -669,9 +719,11 @@
                 spread_weights()
             with jax.named_scope("w_known"):
                 if stages:
-                    hear(len(stages) - 1)
+                    hear(len(stages) - 2)
+                    pass_on(len(stages) - 1)
             with jax.named_scope("st_geo"):
-                start_geometry(knowledge[1], rows)
+                if stages:
+                    start_geometry(False, True)
         else:
             drain_now()
         own_rim(once, double)
@@ -694,6 +746,8 @@
             density = jnp.where(live, density, 0.0).astype(jnp.bfloat16)
             density_out[r] = density
             density_all[r, me] = density
+        if r == 0 and stages:
+            hear(len(stages) - 1)
         with jax.named_scope(f"st_dens{r}"):
             start_gather(density_out.at[r], density_all.at[r], density_recv.at[r, here[0]])
         if r < ROUNDS - 1:
@@ -790,7 +844,7 @@
             pltpu.VMEM((1, 1), jnp.int32),
             pltpu.VMEM((1, slots), jnp.int32),
             pltpu.VMEM(panel_geometry.shape, jnp.float32),
-            pltpu.SemaphoreType.REGULAR((max(1, len(known_stages(rows))),)),
+            pltpu.SemaphoreType.REGULAR((max(1, len(relays(sizes))),)),
             pltpu.SemaphoreType.DMA((7,)),
             pltpu.SemaphoreType.DMA((1,)),
             pltpu.SemaphoreType.DMA((5,)),

time: 27.6 us -> 27.3 us (0.989)
  Pallas kernels: 26.1 us -> 25.8 us
    pallas_call x1, Pallas kernels: 25.4 us -> 25.1 us  [local(): pl.pallas_call(functools.partial(kernel, sizes), out_shape=(jax.ShapeDtyp...]
where the time goes in v6:
time: 27.3 us; the launch traced here: 27.1 us
  Pallas kernels  25.8 us (95%)
  between operations  1.29 us (5%)
    pallas_call x1, Pallas kernels, local(): pl.pallas_call(functools.partial(kernel, sizes), out_shape=(jax.ShapeDtyp...  25.1 us
    pallas_call x1, Pallas kernels, local(): pl.pallas_call(place, out_shape=(jax.ShapeDtypeStruct(initial_field.shape...  0.71 us

profile of v6, /device:TPU:0, one launch (start us, length us, event | category | flops | bytes accessed | tf_op | source)
XLA Modules:
  0.0 27.1 jit_solution(8312054485958364111)
XLA Ops:
  1.3 25.1 %shard_map.86 = (f32[4,16,8,128]{3,2,1,0:T(8,128)S(1)}, f32[8,128]{1,0:T(8,128)S(1)}) custom-call(f32[8,4,16,128]{3,2,1,0:T(8,128)} %init_hbm.1, f32[8,4,16,128]{3,2,1,0:T(8,128)} %source_hbm.1, s32[4,16,128]{2,1,0:T(8,128)} %class_hbm.1, f32[16]{0:T(128)} %shift_hbm.1, s32[1,128]{1,0:T(1,128)} %bitcast.3, s32[1,1]{1,0:T(1,128)} %bitcast.2.live_hbm, ...), custom_call_target="tpu_custom_call" | custom-call | tf_op jit(solution)/shard_map/pallas_call | solution.py:800
  26.4 0.7 %shard_map.87 = (f32[8,4,16,128]{3,2,1,0:T(8,128)}, f32[8,128]{1,0:T(8,128)}) custom-call(f32[4,16,8,128]{3,2,1,0:T(8,128)S(1)} %get-tuple-element.4.field_v, f32[8,128]{1,0:T(8,128)S(1)} %get-tuple-element.5.potential_v), custom_call_target="tpu_custom_call" | custom-call | tf_op jit(solution)/shard_map/pallas_call | solution.py:859

commit v7 on v6

--- a/solution.py
+++ b/solution.py
@@ -69,6 +69,9 @@
         for x in everyone:
             ahead = {at(x, (r, c, d)) for r in (-1, 0, 1) for c in (0, 1) for d in (0, 1) if abs(r) + c + d < 3}
             ahead |= {at(x, (r, 0, 0)) for r in (-2, 2)}
+            if i > 0:
+                ahead |= {at(x, (r, c, d)) for r in (-2, 2) for c in (0, 1) for d in (0, 1)}
+                ahead |= {at(x, (r, 0, 0)) for r in (-4, 4)}
             if i == len(stages) - 2:
                 ahead = {y for y in everyone if (y[0] - x[0]) % 2 == 0}
             if i == len(stages) - 1:
@@ -108,9 +111,6 @@
     def brick_wait(vmem, sem):
         pltpu.make_async_copy(vmem, vmem, sem).wait()
 
-    for copy in brick_copies(init_hbm, init_v, local_sem.at[0]):
-        copy.start()
-
     stages = relays(sizes)
     barrier = pltpu.get_barrier_semaphore()
 
@@ -157,6 +157,9 @@
         near = tellers(0)
     else:
         near = devices - 1
+
+    for copy in brick_copies(init_hbm, init_v, local_sem.at[0]):
+        copy.start()
 
     copies = [
         pltpu.make_async_copy(class_hbm, class_v, local_sem.at[1]),
@@ -373,16 +376,14 @@
 
     others_beside = [(b, c) for b in range(cols) for c in range(depths)]
 
-    def start_geometry(near_part, far_part):
-        if near_part:
+    def start_geometry(*parts):
+        if 0 in parts:
             for b, c in others_beside[1:]:
                 send_geometry(here[0], b, c)
         for away in reversed(range(fold, rows, fold)):
-            targets = []
-            if near_part and away == fold or far_part and away > fold:
-                targets += others_beside[:1]
-            if far_part:
-                targets += others_beside[1:]
+            step = min(away // fold, 3)
+            targets = others_beside[:1] if step - 1 in parts else []
+            targets = targets + (others_beside[1:] if min(step, 2) in parts else [])
 
             def to_row(row, targets=targets):
                 for b, c in targets:
@@ -586,6 +587,7 @@
                 around = around + corner_xy(q, 1, side)
             return rim_y[side, x] + from_y(q + 1, side, x) + rim_wy[side, x] * around
 
+        cells = []
         for x in range(size_x):
             for p in range(pairs):
                 below = swept_x(0, p) if x == 0 else None
@@ -600,7 +602,16 @@
                         around = around + swept_y(0, x)
                     if y == size_y - 1:
                         around = around + swept_y(1, x)
-                    target[x, y] = target[x, y] + weight_v[x, y] * around
+                    cell = target[x, y] + weight_v[x, y] * around
+                    target[x, y] = cell
+                    cells.append(cell)
+        return cells
+
+    def sum_up(found):
+        sums = [block * at_cell[at] for at, block in enumerate(found)]
+        while len(sums) > 1:
+            sums = [a + b for a, b in zip(sums[::2], sums[1::2])]
+        return sums[0]
 
     pieces = 4
     chunk = slots // pieces
@@ -672,14 +683,21 @@
                 make_tiles()
         if r == 0:
             with jax.named_scope("w_known0"):
+                early = stages[1:-2]
                 if stages:
                     hear(0)
                     pass_on(1)
-                start_geometry(True, not stages)
+                    start_geometry(0)
+                    if early:
+                        hear(1)
+                        pass_on(2)
+                        start_geometry(1)
+                else:
+                    start_geometry(0, 1, 2)
         with jax.named_scope(f"w_single{r}"):
             land(0, face_cells)
         if r == 0 and stages:
-            for stage in range(1, len(stages) - 2):
+            for stage in range(2, len(stages) - 2):
                 hear(stage)
                 pass_on(stage + 1)
         with jax.named_scope(f"outer{r}"):
@@ -723,7 +741,7 @@
                     pass_on(len(stages) - 1)
             with jax.named_scope("st_geo"):
                 if stages:
-                    start_geometry(False, True)
+                    start_geometry(*((2,) if early else (1, 2)))
         else:
             drain_now()
         own_rim(once, double)
@@ -737,12 +755,9 @@
         with jax.named_scope(f"w_rim{r}"):
             land(2, face_cells)
         with jax.named_scope(f"rim{r}"):
-            rim(after, double)
-        with jax.named_scope(f"density{r}"):
-            flat = after[...].reshape(size_x * size_y * channels, size_z).astype(jnp.bfloat16)
-            picked = jnp.dot(flat, pick_z, preferred_element_type=jnp.float32)
-            picked = picked.reshape(size_x * size_y, channels, slots)
-            density = jnp.sum(picked * at_cell[...], axis=0)
+            cells = rim(after, double)
+            parts = [jnp.dot(jnp.concatenate(cells[x * size_y : (x + 1) * size_y], axis=0).astype(jnp.bfloat16), pick_z, preferred_element_type=jnp.float32) for x in range(size_x)]
+            density = sum_up([found[channels * i : channels * (i + 1)] for found in parts for i in range(found.shape[0] // channels)])
             density = jnp.where(live, density, 0.0).astype(jnp.bfloat16)
             density_out[r] = density
             density_all[r, me] = density

time: 27.3 us -> 27.2 us (level)
  no operation moved by 1% of the time
where the time goes in v7:
time: 27.2 us; the launch traced here: 27 us
  Pallas kernels  25.7 us (94%)
  between operations  1.29 us (5%)
    pallas_call x1, Pallas kernels, local(): pl.pallas_call(functools.partial(kernel, sizes), out_shape=(jax.ShapeDtyp...  25 us
    pallas_call x1, Pallas kernels, local(): pl.pallas_call(place, out_shape=(jax.ShapeDtypeStruct(initial_field.shape...  0.71 us

profile of v7, /device:TPU:0, one launch (start us, length us, event | category | flops | bytes accessed | tf_op | source)
XLA Modules:
  0.0 27.0 jit_solution(16600350730627367501)
XLA Ops:
  1.3 25.0 %shard_map.86 = (f32[4,16,8,128]{3,2,1,0:T(8,128)S(1)}, f32[8,128]{1,0:T(8,128)S(1)}) custom-call(f32[8,4,16,128]{3,2,1,0:T(8,128)} %init_hbm.1, f32[8,4,16,128]{3,2,1,0:T(8,128)} %source_hbm.1, s32[4,16,128]{2,1,0:T(8,128)} %class_hbm.1, f32[16]{0:T(128)} %shift_hbm.1, s32[1,128]{1,0:T(1,128)} %bitcast.3, s32[1,1]{1,0:T(1,128)} %bitcast.2.live_hbm, ...), custom_call_target="tpu_custom_call" | custom-call | tf_op jit(solution)/shard_map/pallas_call | solution.py:815
  26.3 0.7 %shard_map.87 = (f32[8,4,16,128]{3,2,1,0:T(8,128)}, f32[8,128]{1,0:T(8,128)}) custom-call(f32[4,16,8,128]{3,2,1,0:T(8,128)S(1)} %get-tuple-element.4.field_v, f32[8,128]{1,0:T(8,128)S(1)} %get-tuple-element.5.potential_v), custom_call_target="tpu_custom_call" | custom-call | tf_op jit(solution)/shard_map/pallas_call | solution.py:874

commit v8 on v7

--- a/solution.py
+++ b/solution.py
@@ -91,7 +91,7 @@
     rim_wx, rim_wy, rim_wz, meter,
     geo_all, column_v, tile_v, density_out, density_all, at_cell,
     shift_ref, live_ref, cell_ref, geo_ref,
-    known, local_sem, face_send, face_recv, gather_send, geo_recv, density_recv,
+    known, local_sem, face_send, face_recv, gather_send, geo_relay, geo_recv, density_recv,
 ):
     rows, cols, depths = sizes
     devices = rows * cols * depths
@@ -364,12 +364,14 @@
     fold = 2 - rows % 2
     layers, layer, part = rows // fold, here[0] // fold, lax.rem(here[0], fold)
 
-    def send_geometry(row, b, c):
+    handed_on = len(stages) > 3 and layers <= 4
+
+    def send_geometry(row, b, c, sem=None):
         pltpu.make_async_remote_copy(
             src_ref=geo_ref,
             dst_ref=geo_all.at[me],
             send_sem=gather_send.at[0],
-            recv_sem=geo_recv.at[here[0]],
+            recv_sem=geo_recv.at[here[0]] if sem is None else sem,
             device_id=(row, lax.rem(here[1] + b, cols), lax.rem(here[2] + c, depths)),
             device_id_type=MESH,
         ).start()
@@ -382,16 +384,69 @@
                 send_geometry(here[0], b, c)
         for away in reversed(range(fold, rows, fold)):
             step = min(away // fold, 3)
-            targets = others_beside[:1] if step - 1 in parts else []
-            targets = targets + (others_beside[1:] if min(step, 2) in parts else [])
-
-            def to_row(row, targets=targets):
+            down = others_beside[:1] if step - 1 in parts else []
+            down = down + (others_beside[1:] if min(step, 2) in parts else [])
+            up, sem = down, None
+            if handed_on and step > 1:
+                up, sem = (others_beside[:1] if step == 2 and 1 in parts else []), geo_relay.at[0]
+
+            def to_row(row, targets, sem):
                 for b, c in targets:
-                    send_geometry(row, b, c)
-
-            if targets:
-                pl.when(here[0] >= away)(lambda: to_row(here[0] - away))
-                pl.when(here[0] + away < rows)(lambda: to_row(here[0] + away))
+                    send_geometry(row, b, c, sem)
+
+            if down:
+                pl.when(here[0] >= away)(
+                    functools.partial(to_row, here[0] - away, down, None)
+                )
+            if up:
+                pl.when(here[0] + away < rows)(
+                    functools.partial(to_row, here[0] + away, up, sem)
+                )
+
+    def hand_on():
+        def pass_block(q, onward):
+            block = geo_all.at[(q * cols + here[1]) * depths + here[2]]
+            pltpu.make_async_copy(block, block, geo_relay.at[0]).wait()
+
+            def send(row, b, c):
+                pltpu.make_async_remote_copy(
+                    src_ref=block,
+                    dst_ref=block,
+                    send_sem=gather_send.at[0],
+                    recv_sem=geo_recv.at[q],
+                    device_id=(
+                        row, lax.rem(here[1] + b, cols), lax.rem(here[2] + c, depths)
+                    ),
+                    device_id_type=MESH,
+                ).start()
+
+            def send_onward():
+                for b, c in others_beside:
+                    send(onward, b, c)
+
+            pl.when(onward < rows)(send_onward)
+            for b, c in others_beside[1:]:
+                send(here[0], b, c)
+
+        two = 2 * fold
+        pl.when(here[0] >= two)(lambda: pass_block(here[0] - two, here[0] + fold))
+
+    def drain_geometry():
+        def spent(count, present=None):
+            when(present, lambda: await_gather(geo_all, count, gather_send.at[0]))
+
+        if not handed_on:
+            spent(devices - 1)
+            return
+        spent(layers * group)
+        spent(group - 1)
+        for n in range(1, layers):
+            spent(group, here[0] >= n * fold)
+            if n < 3:
+                spent(group if n == 1 else 1, here[0] + n * fold < rows)
+        two = 2 * fold
+        spent(group - 1, here[0] >= two)
+        spent(group, (here[0] >= two) & (here[0] + fold < rows))
 
     def hand_over(q):
         blocks = geo_all.at[pl.ds(q * group, group)]
@@ -620,7 +675,15 @@
         def body(i, carry):
             a, k = i // layers, lax.rem(i, layers)
             q = nearest(k, layer, layers) * fold + lax.rem(part + a, fold)
-            await_gather(geo_all, group, geo_recv.at[q])
+            if handed_on:
+                away = q // fold - layer
+                relayed = (a == 0) & (away == -2)
+                pl.when(relayed)(lambda: await_gather(geo_all, group - 1, geo_recv.at[q]))
+                pl.when(jnp.logical_not(relayed))(
+                    lambda: await_gather(geo_all, group, geo_recv.at[q])
+                )
+            else:
+                await_gather(geo_all, group, geo_recv.at[q])
             if fold > 1:
                 pl.when(a == 0)(lambda: hand_over(q))
             for j in range(group):
@@ -665,7 +728,7 @@
             if q % 3 == 1:
                 drain(edge_cells)
         drain(weight_cells)
-        await_gather(geo_all, devices - 1, gather_send.at[0])
+        drain_geometry()
         for r in range(ROUNDS - 1):
             await_gather(density_all.at[r], devices - 1, gather_send.at[0])
 
@@ -742,6 +805,8 @@
             with jax.named_scope("st_geo"):
                 if stages:
                     start_geometry(*((2,) if early else (1, 2)))
+                if handed_on:
+                    hand_on()
         else:
             drain_now()
         own_rim(once, double)
@@ -864,6 +929,7 @@
             pltpu.SemaphoreType.DMA((1,)),
             pltpu.SemaphoreType.DMA((5,)),
             pltpu.SemaphoreType.DMA((1,)),
+            pltpu.SemaphoreType.DMA((1,)),
             pltpu.SemaphoreType.DMA((rows,)),
             pltpu.SemaphoreType.DMA((ROUNDS, rows)),
         ],

time: 27.2 us -> 27 us (level)
  no operation moved by 1% of the time
where the time goes in v8:
time: 27 us; the launch traced here: 26.8 us
  Pallas kernels  25.5 us (94%)
  between operations  1.29 us (5%)
    pallas_call x1, Pallas kernels, local(): pl.pallas_call(functools.partial(kernel, sizes), out_shape=(jax.ShapeDtyp...  24.8 us
    pallas_call x1, Pallas kernels, local(): pl.pallas_call(place, out_shape=(jax.ShapeDtypeStruct(initial_field.shape...  0.71 us

profile of v8, /device:TPU:0, one launch (start us, length us, event | category | flops | bytes accessed | tf_op | source)
XLA Modules:
  0.0 26.8 jit_solution(4108723803722651857)
XLA Ops:
  1.3 24.8 %shard_map.86 = (f32[4,16,8,128]{3,2,1,0:T(8,128)S(1)}, f32[8,128]{1,0:T(8,128)S(1)}) custom-call(f32[8,4,16,128]{3,2,1,0:T(8,128)} %init_hbm.1, f32[8,4,16,128]{3,2,1,0:T(8,128)} %source_hbm.1, s32[4,16,128]{2,1,0:T(8,128)} %class_hbm.1, f32[16]{0:T(128)} %shift_hbm.1, s32[1,128]{1,0:T(1,128)} %bitcast.3, s32[1,1]{1,0:T(1,128)} %bitcast.2.live_hbm, ...), custom_call_target="tpu_custom_call" | custom-call | tf_op jit(solution)/shard_map/pallas_call | solution.py:880
  26.1 0.7 %shard_map.87 = (f32[8,4,16,128]{3,2,1,0:T(8,128)}, f32[8,128]{1,0:T(8,128)}) custom-call(f32[4,16,8,128]{3,2,1,0:T(8,128)S(1)} %get-tuple-element.4.field_v, f32[8,128]{1,0:T(8,128)S(1)} %get-tuple-element.5.potential_v), custom_call_target="tpu_custom_call" | custom-call | tf_op jit(solution)/shard_map/pallas_call | solution.py:940

commit v9 on v8

--- a/solution.py
+++ b/solution.py
@@ -100,6 +100,7 @@
     slots = cell_hbm.shape[1]
     classes = shift_ref.shape[0]
     factor = 1.0 / math.sqrt(slots * devices)
+    per_turn = wave_number / (2.0 * math.pi)
     here = tuple(lax.axis_index(axis) for axis in AXES)
     me = (here[0] * cols + here[1]) * depths + here[2]
 
@@ -357,7 +358,7 @@
     )
     for i in range(3):
         column = jnp.sum(jnp.where(eye, geo_ref[i : i + 1, :], 0.0), axis=1, keepdims=True)
-        column_v[i] = jnp.broadcast_to(column, (slots, slots))
+        column_v[i] = jnp.broadcast_to(column * per_turn, (slots, slots))
     pltpu.make_async_copy(geo_ref, geo_all.at[me], geo_recv.at[here[0]]).start()
 
 
@@ -687,16 +688,16 @@
             if fold > 1:
                 pl.when(a == 0)(lambda: hand_over(q))
             for j in range(group):
-                source = geo_all[q * group + j]
+                source = geo_all[q * group + j] * per_turn
                 for piece in range(pieces):
                     span = slice(piece * chunk, (piece + 1) * chunk)
                     delta_x = column_v[0, span, :] - source[0:1, :]
                     delta_y = column_v[1, span, :] - source[1:2, :]
                     delta_z = column_v[2, span, :] - source[2:3, :]
                     square = delta_x * delta_x + delta_y * delta_y + delta_z * delta_z + 1e-30
-                    distance = square * lax.rsqrt(square)
-                    wave = cosine_of_turns(distance * (wave_number / (2.0 * math.pi)))
-                    value = (source[3:4, :] * factor) * wave / (distance + soften)
+                    turns = square * lax.rsqrt(square)
+                    wave = cosine_of_turns(turns)
+                    value = (source[3:4, :] * factor) * wave / (turns + soften * per_turn)
                     tile_v[q, span, j * slots : (j + 1) * slots] = value.astype(tile_v.dtype)
             return carry
 

time: 27 us -> 27 us (level)
  no operation moved by 1% of the time
where the time goes in v9:
time: 27 us; the launch traced here: 26.8 us
  Pallas kernels  25.5 us (94%)
  between operations  1.29 us (5%)
    pallas_call x1, Pallas kernels, local(): pl.pallas_call(functools.partial(kernel, sizes), out_shape=(jax.ShapeDtyp...  24.8 us
    pallas_call x1, Pallas kernels, local(): pl.pallas_call(place, out_shape=(jax.ShapeDtypeStruct(initial_field.shape...  0.71 us

profile of v9, /device:TPU:0, one launch (start us, length us, event | category | flops | bytes accessed | tf_op | source)
XLA Modules:
  0.0 26.8 jit_solution(7033587849170827225)
XLA Ops:
  1.3 24.8 %shard_map.86 = (f32[4,16,8,128]{3,2,1,0:T(8,128)S(1)}, f32[8,128]{1,0:T(8,128)S(1)}) custom-call(f32[8,4,16,128]{3,2,1,0:T(8,128)} %init_hbm.1, f32[8,4,16,128]{3,2,1,0:T(8,128)} %source_hbm.1, s32[4,16,128]{2,1,0:T(8,128)} %class_hbm.1, f32[16]{0:T(128)} %shift_hbm.1, s32[1,128]{1,0:T(1,128)} %bitcast.3, s32[1,1]{1,0:T(1,128)} %bitcast.2.live_hbm, ...), custom_call_target="tpu_custom_call" | custom-call | tf_op jit(solution)/shard_map/pallas_call | solution.py:881
  26.1 0.7 %shard_map.87 = (f32[8,4,16,128]{3,2,1,0:T(8,128)}, f32[8,128]{1,0:T(8,128)}) custom-call(f32[4,16,8,128]{3,2,1,0:T(8,128)S(1)} %get-tuple-element.4.field_v, f32[8,128]{1,0:T(8,128)S(1)} %get-tuple-element.5.potential_v), custom_call_target="tpu_custom_call" | custom-call | tf_op jit(solution)/shard_map/pallas_call | solution.py:941
